TPU v7x, 8 devices: a whole 2x2x1 slice. The times are simulated.
8 devices in a mesh: dp: 1 (over z), tp: 2 (over y), cp: 4 (over x, core).
Axes of the slice: x: 2, y: 2, z: 1, core: 2. Of those that a mesh axis runs over, the one named last changes fastest.
Arguments:
- hidden: bfloat16 [32, 32, 2048], P('dp')
- prefix_len: int32 [32], P('dp')
- k_cache: bfloat16 [32, 8192, 8, 128], P('dp', 'cp', 'tp')
- v_cache: bfloat16 [32, 8192, 8, 128], P('dp', 'cp', 'tp')
- attn_norm: bfloat16 [2048], replicated
- w_q: bfloat16 [2048, 2048], P(None, 'tp')
- w_k: bfloat16 [2048, 1024], P(None, 'tp')
- w_v: bfloat16 [2048, 1024], P(None, 'tp')
- w_o: bfloat16 [2048, 2048], P('tp')
- q_norm: bfloat16 [128], replicated
- k_norm: bfloat16 [128], replicated
Outputs:
- output 1: bfloat16 [32, 32, 2048], P('dp')
- output 2: bfloat16 [32, 32, 8, 128], P('dp', None, 'tp')
- output 3: bfloat16 [32, 32, 8, 128], P('dp', None, 'tp')
All inputs are finite; a program needn't handle non-finite values.
Results may differ from a plain program's by a relative error of at most 0.00372417.
Values sent between devices are 32-bit elements.
A program may use at most 1 GiB of HBM per device.

v0:
```python
import jax
import jax.numpy as jnp
from jax import lax
from jax.sharding import PartitionSpec as P

HEAD_DIM = 128
MASKED = -1e30


def rms_scale(tensor, norm_gain):
    mean_sq = jnp.mean(jnp.square(tensor), axis=-1, keepdims=True)
    return tensor * lax.rsqrt(mean_sq + 1e-6) * norm_gain


def rope_apply(tensor, positions):
    half_dim = HEAD_DIM // 2
    inv_freq = 1.0 / (1000000.0 ** (jnp.arange(half_dim, dtype=jnp.float32) * 2.0 / HEAD_DIM))
    angles = positions.astype(jnp.float32)[..., None] * inv_freq
    cos_t = jnp.cos(angles)[..., None, :]
    sin_t = jnp.sin(angles)[..., None, :]
    lead_half = tensor[..., :half_dim]
    tail_half = tensor[..., half_dim:]
    return jnp.concatenate([lead_half * cos_t - tail_half * sin_t, tail_half * cos_t + lead_half * sin_t], axis=-1)


def project_new(hidden, attn_norm, w_q, w_k, w_v, q_norm, k_norm, prefix_len):
    n_seq, n_new, d_model = hidden.shape
    kv_count = w_k.shape[1] // HEAD_DIM
    head_count = w_q.shape[1] // HEAD_DIM
    normed = rms_scale(hidden.astype(jnp.float32), attn_norm.astype(jnp.float32)).astype(jnp.bfloat16)
    q_lin = jnp.einsum('bce,ef->bcf', normed, w_q, preferred_element_type=jnp.float32).astype(jnp.bfloat16)
    k_lin = jnp.einsum('bce,ef->bcf', normed, w_k, preferred_element_type=jnp.float32).astype(jnp.bfloat16)
    v_lin = jnp.einsum('bce,ef->bcf', normed, w_v, preferred_element_type=jnp.float32).astype(jnp.bfloat16)
    positions = prefix_len[:, None] + jnp.arange(n_new, dtype=jnp.int32)[None, :]
    q_heads = q_lin.reshape(n_seq, n_new, head_count, HEAD_DIM).astype(jnp.float32)
    k_heads = k_lin.reshape(n_seq, n_new, kv_count, HEAD_DIM).astype(jnp.float32)
    q_rot = rope_apply(rms_scale(q_heads, q_norm.astype(jnp.float32)), positions).astype(jnp.bfloat16)
    k_new = rope_apply(rms_scale(k_heads, k_norm.astype(jnp.float32)), positions).astype(jnp.bfloat16)
    v_new = v_lin.reshape(n_seq, n_new, kv_count, HEAD_DIM)
    q_grp = q_rot.reshape(n_seq, n_new, kv_count, head_count // kv_count, HEAD_DIM)
    return q_grp, k_new, v_new


def attend_partial(q_grp, k_cache, v_cache, k_new, v_new, slot_ok, own_ok):
    score_scale = HEAD_DIM ** -0.5
    s_cache = jnp.einsum('bckgd,bpkd->bkcgp', q_grp, k_cache, preferred_element_type=jnp.float32) * score_scale
    s_cache = jnp.where(slot_ok[:, None, None, None, :], s_cache, MASKED)
    s_own = jnp.einsum('bckgd,bikd->bkcgi', q_grp, k_new, preferred_element_type=jnp.float32) * score_scale
    s_own = jnp.where(own_ok[None, None, :, None, :], s_own, MASKED)
    row_max = jnp.maximum(jnp.max(s_cache, axis=-1), jnp.max(s_own, axis=-1))
    p_cache = jnp.exp(s_cache - row_max[..., None])
    p_own = jnp.exp(s_own - row_max[..., None])
    row_sum = jnp.sum(p_cache, axis=-1) + jnp.sum(p_own, axis=-1)
    weighted = jnp.einsum('bkcgp,bpkd->bkcgd', p_cache.astype(jnp.bfloat16), v_cache, preferred_element_type=jnp.float32)
    weighted = weighted + jnp.einsum('bkcgi,bikd->bkcgd', p_own.astype(jnp.bfloat16), v_new, preferred_element_type=jnp.float32)
    return row_max, row_sum, weighted


def out_partial(attn_out, w_o):
    kv_count = attn_out.shape[1]
    group_size = attn_out.shape[3]
    w_heads = w_o.reshape(kv_count, group_size, HEAD_DIM, w_o.shape[1])
    return jnp.einsum('bkcgd,kgde->bce', attn_out, w_heads, preferred_element_type=jnp.float32)


def solution(mesh):
    def per_device(hidden, prefix_len, k_cache, v_cache, attn_norm, w_q, w_k, w_v, w_o, q_norm, k_norm):
        n_new = hidden.shape[1]
        cache_slots = k_cache.shape[1]
        cp_index = lax.axis_index('cp')
        q_grp, k_new, v_new = project_new(hidden, attn_norm, w_q, w_k, w_v, q_norm, k_norm, prefix_len)
        slot_ids = cp_index * cache_slots + jnp.arange(cache_slots)
        slot_ok = slot_ids[None, :] < prefix_len[:, None]
        new_ids = jnp.arange(n_new)
        own_ok = (new_ids[:, None] >= new_ids[None, :]) & (cp_index == 0)
        row_max, row_sum, weighted = attend_partial(q_grp, k_cache, v_cache, k_new, v_new, slot_ok, own_ok)
        glob_max = lax.pmax(row_max, 'cp')
        factor = jnp.exp(row_max - glob_max)
        total_w, total_sum = lax.psum((weighted * factor[..., None], row_sum * factor), 'cp')
        attn_out = (total_w / total_sum[..., None]).astype(jnp.bfloat16)
        out_proj = lax.psum(out_partial(attn_out, w_o), 'tp')
        block_out = (hidden.astype(jnp.float32) + out_proj).astype(jnp.bfloat16)
        return block_out, k_new, v_new

    cache_spec = P('dp', 'cp', 'tp', None)
    arg_specs = (P('dp', None, None), P('dp'), cache_spec, cache_spec, P(None), P(None, 'tp'), P(None, 'tp'), P(None, 'tp'), P('tp', None), P(None), P(None))
    out_specs = (P('dp', None, None), P('dp', None, 'tp', None), P('dp', None, 'tp', None))
    return jax.shard_map(per_device, mesh=mesh, in_specs=arg_specs, out_specs=out_specs, check_vma=False)
```

profile of v0, /device:TPU:0, one launch (start us, length us, event | category | flops | bytes accessed | tf_op | source)
XLA Modules:
  0.0 508.8 jit_solution(9755296444111709802)
XLA Ops:
  7.2 0.0 copy-start
  7.2 0.0 all-reduce.3.cloned.1.call-start
  7.2 0.0 copy-start.2
  7.3 3.2 fusion.8
  10.5 0.8 copy-done.2
  11.3 3.7 fusion.40
  15.0 2.1 reshape.129
  17.1 1.2 multiply_reduce_fusion
  18.3 0.3 copy.34
  18.7 0.1 add_convert_fusion.2
  18.7 7.6 %convert_convert_fusion = f32[32,32,1024]{2,1,0:T(8,128)S(1)} fusion(bf16[2048,1024]{1,0:T(8,128)(2,1)} %param.16, bf16[32,32,2048]{2,1,0:T(8,128)(2,1)} %param.11, f32[2048]{0:T(1024)S(1)} %convert_element_type.61, f32[32,32]{1,0:T(8,128)S(1)} %add_rsqrt_fusion.2), kind=kOutput, calls=%fused_computation.47 | convolution fusion | flops 4305453056 | bytes 12595200 | tf_op jit(solution)/shard_map/bce,ef->bcf/dot_general | solution.py:31
  26.4 1.0 copy.63
  27.4 0.0 copy-start.12
  27.4 0.0 copy-start.6
  27.4 1.1 fusion.12
  28.6 0.1 add_rsqrt_fusion
  28.7 0.3 copy-done.6
  29.0 0.7 fusion.26
  29.7 1.9 multiply_cosine_fusion
  31.6 2.0 subtract_convert_fusion.1
  33.6 1.2 fusion.13
  34.8 1.9 subtract_convert_fusion
  36.8 0.5 copy.31
  37.3 1.8 copy.32
  39.1 0.1 broadcast_compare_fusion
  39.2 1.8 pad_maximum_fusion.1
  41.0 7.5 %fusion.18 = (f32[32,4,32,2]{2,3,1,0:T(2,128)S(1)}, f32[32,4,32,2,32]{2,4,3,1,0:T(8,128)}) fusion(pred[32,32]{0,1:T(8,128)(4,1)S(1)} %fusion.53, bf16[32,32,4,128]{3,1,2,0:T(8,128)(2,1)S(1)} %pad_maximum_fusion.1, bf16[32,32,4,2,64]{4,1,3,2,0:T(8,128)(2,1)} %bitcast.70, bf16[32,32,4,2,64]{4,1,3,2,0:T(8,128)(2,1)S(1)} %bitcast.68), kind=kOutput, calls=%fused_computation.32 | convolution fusion | flops 72081408 | bytes 4228096 | tf_op jit(solution)/shard_map/bckgd,bikd->bkcgi/dot_general | solution.py:48
  48.6 54.5 %fusion.4 = (f32[32,4,32,2]{2,3,1,0:T(2,128)S(1)}, f32[32,4,32,2,2048]{4,2,3,1,0:T(8,128)}) fusion(pred[32,2048]{1,0:T(8,128)(4,1)S(1)} %broadcast_compare_fusion, bf16[32,2048,4,128,1]{3,2,1,0,4:T(4,128)(2,1)} %bitcast.3, bf16[32,32,4,2,64]{4,1,3,2,0:T(8,128)(2,1)} %bitcast.71, bf16[32,32,4,2,64]{4,1,3,2,0:T(8,128)(2,1)S(1)} %bitcast.69), kind=kOutput, calls=%fused_computation.6 | convolution fusion | flops 4349485056 | bytes 136413184 | tf_op jit(solution)/shard_map/bckgd,bpkd->bkcgp/dot_general | solution.py:46
  103.1 0.1 max.9
  103.2 15.6 %pmax.7 = f32[32,4,32,2]{2,3,1,0:T(2,128)} all-reduce(f32[32,4,32,2]{2,3,1,0:T(2,128)S(1)} %max.9), channel_id=1, replica_groups=mesh['dp'=1,'tp'=2,'cp'=4] {'cp'}, use_global_device_ids=true, to_apply=%region_5.6 | all-reduce | flops 8192 | bytes 65536 | tf_op jit(solution)/shard_map/pmax | solution.py:77
  118.8 4.6 fusion.19
  123.4 33.5 %fusion.5 = (f32[32,4,32,2]{2,3,1,0:T(2,128)S(1)}, bf16[32,4,32,2,2048]{4,2,3,1,0:T(8,128)(2,1)}) fusion(f32[32,4,32,2,2048]{4,2,3,1,0:T(8,128)} %get-tuple-element.25, f32[32,4,32,2]{2,3,1,0:T(2,128)S(1)} %max.9, pred[32,2048]{1,0:T(8,128)(4,1)S(1)} %broadcast_compare_fusion), kind=kLoop, calls=%fused_computation.7 | loop fusion | flops 83877888 | bytes 100794368 | tf_op jit(solution)/shard_map/reduce_sum | solution.py:53
  156.9 1.6 add_multiply_fusion.1
  158.6 5.0 fusion.45
  163.6 1.3 reshape.126
  164.9 38.2 %fusion = f32[32,4,32,2,128]{4,2,1,3,0:T(8,128)} fusion(bf16[32,2048,4,128,1]{3,2,1,0,4:T(4,128)(2,1)} %bitcast.7, bf16[32,4,32,2,2048]{4,2,3,1,0:T(8,128)(2,1)} %get-tuple-element.15), kind=kOutput, calls=%fused_computation | convolution fusion | flops 4294967296 | bytes 104857600 | tf_op jit(solution)/shard_map/bkcgp,bpkd->bkcgd/dot_general | solution.py:54
  203.1 6.1 %add_multiply_fusion = f32[32,4,32,2,128]{4,2,1,3,0:T(8,128)} fusion(f32[32,4,32,2,128]{4,2,1,3,0:T(8,128)} %fusion, bf16[32,4,32,2,32]{2,4,3,1,0:T(8,128)(2,1)S(1)} %get-tuple-element.19, f32[32,4,32,2]{2,1,3,0:T(4,128)S(1)} %copy.41, bf16[32,32,4,128,1]{3,2,1,0,4:T(4,128)(2,1)S(1)} %bitcast.72), kind=kOutput, calls=%fused_computation.27 | convolution fusion | flops 69206016 | bytes 9994240 | tf_op jit(solution)/shard_map/bkcgi,bikd->bkcgd/dot_general | solution.py:55
  209.2 0.0 all-reduce.3.cloned.1.call-update
  209.2 0.0 all-reduce.5.cloned.1.call-start
  209.3 0.8 copy-done.8
  210.1 15.5 %psum.22 = f32[32,4,32,2]{2,3,1,0:T(2,128)S(1)} all-reduce(f32[32,4,32,2]{2,3,1,0:T(2,128)S(1)} %bitcast.77), channel_id=1, replica_groups=mesh['dp'=1,'tp'=2,'cp'=4] {'cp'}, use_global_device_ids=true, to_apply=%region_9.10 | all-reduce | flops 8192 | bytes 65536 | tf_op jit(solution)/shard_map/psum | solution.py:79
  225.7 65.6 %all-reduce.3.cloned.1.call-done = f32[32,4,32,2,128]{4,2,1,3,0:T(8,128)} async-done(((f32[32,4,32,2,128]{4,2,1,3,0:T(8,128)}), f32[32,4,32,2,128]{4,2,1,3,0:T(8,128)}) %all-reduce.3.cloned.1.call-update) | async-done | bytes 4194320 | tf_op jit(solution)/shard_map/psum | solution.py:79
  291.3 9.6 %convolution_bitcast_fusion = f32[32,32,2048]{2,1,0:T(8,128)} fusion(bf16[4,2,128,2048,1]{3,2,1,0,4:T(8,128)(2,1)} %bitcast.80, f32[32,4,32,2,128]{4,2,1,3,0:T(8,128)} %all-reduce.3.cloned.1.call-done, f32[32,4,32,2]{2,1,3,0:T(4,128)S(1)} %copy.42), kind=kOutput, calls=%fused_computation.17 | convolution fusion | flops 4297064448 | bytes 16809984 | tf_op jit(solution)/shard_map/bkcgd,kgde->bce/dot_general | solution.py:63
  300.9 0.0 all-reduce.5.cloned.1.call-update
  300.9 1.2 copy-done.5
  302.1 1.5 copy.45
  303.6 189.8 %all-reduce.5.cloned.1.call-done = f32[32,32,2048]{2,1,0:T(8,128)} async-done(((f32[32,32,2048]{2,1,0:T(8,128)}), f32[32,32,2048]{2,1,0:T(8,128)}) %all-reduce.5.cloned.1.call-update) | async-done | bytes 8388624 | tf_op jit(solution)/shard_map/psum | solution.py:81
  493.4 8.4 %fusion.11 = bf16[32,32,2048]{2,1,0:T(8,128)(2,1)} fusion(f32[32,32,2048]{2,1,0:T(8,128)} %all-reduce.5.cloned.1.call-done, bf16[32,32,2048]{2,1,0:T(8,128)(2,1)} %param.11), kind=kLoop, calls=%fused_computation.16 | loop fusion | flops 6291456 | bytes 16777216 | tf_op jit(solution)/shard_map/convert_element_type | solution.py:82
  (29 shorter events, 0.2 us)
Async XLA Ops:
  7.2 3.4 copy-start
  7.2 3.3 copy-start.9
  7.2 284.1 %all-reduce.3.cloned.1.call-start = ((), (), s32[]{:S(2)}) async-start(), calls=%async_computation | async-start | bytes 8388608 | tf_op jit(solution)/shard_map/psum | solution.py:79
  7.2 4.0 copy-start.2
  15.0 3.7 copy-start.11
  15.0 3.7 copy-start.10
  27.4 1.3 copy-start.12
  27.4 1.6 copy-start.6
  41.0 7.6 %copy-start.4 = (bf16[32,32,4,128]{3,1,2,0:T(8,128)(2,1)}, bf16[32,32,4,128]{3,1,2,0:T(8,128)(2,1)S(1)}, u32[]{:S(2)}) copy-start(bf16[32,32,4,128]{3,1,2,0:T(8,128)(2,1)S(1)} %pad_maximum_fusion.1) | copy-start | bytes 3145732
  123.4 35.2 %copy-start.3 = (bf16[32,32,2048]{2,1,0:T(8,128)(2,1)S(1)}, bf16[32,32,2048]{2,1,0:T(8,128)(2,1)}, u32[]{:S(2)}) copy-start(bf16[32,32,2048]{2,1,0:T(8,128)(2,1)} %param.11) | copy-start | bytes 12582916
  164.9 38.2 %copy-start.7 = (bf16[32,32,4,128]{3,2,1,0:T(4,128)(2,1)}, bf16[32,32,4,128]{3,2,1,0:T(4,128)(2,1)S(1)}, u32[]{:S(2)}) copy-start(bf16[32,32,4,128]{3,2,1,0:T(4,128)(2,1)S(1)} %reshape.126) | copy-start | bytes 3145732
  209.2 0.9 copy-start.8
  209.2 284.2 %all-reduce.5.cloned.1.call-start = ((), (), s32[]{:S(2)}) async-start(), calls=%async_computation.1 | async-start | bytes 16777216 | tf_op jit(solution)/shard_map/psum | solution.py:81
  300.9 1.2 copy-start.5
  493.4 8.4 %copy-start.1 = (bf16[2048,512]{1,0:T(8,128)(2,1)S(1)}, bf16[2048,512]{1,0:T(8,128)(2,1)}, u32[]{:S(2)}) copy-start(bf16[2048,512]{1,0:T(8,128)(2,1)} %param.17) | copy-start | bytes 6291460
Sparse Core Ops, SparseCore 0:
  209.3 81.8 all-reduce.2
  301.0 192.3 all-reduce.4
where the time goes:
time: 513 us; the launch traced here: 509 us
  waiting for transfers between devices  255 us (50%)
  matrix products  132 us (26%)
  other arithmetic  63.7 us (12%)
  blocking collectives  31.2 us (6%)
  between operations  14.5 us (3%)
  local copies, waits for them, and re-layouts  11.8 us (2%)
    psum x1, waiting for transfers between devices, per_device(): out_proj = lax.psum(out_partial(attn_out, w_o), 'tp')  190 us
    psum x1, waiting for transfers between devices, per_device(): lax.psum((weighted * factor[..., None], row_sum * factor), 'cp')  65.6 us
    dot_general x1, matrix products, attend_partial(): jnp.einsum('bckgd,bpkd->bkcgp', q_grp, k_cache, preferred_element_type=jn...  54.5 us
    dot_general x1, matrix products, attend_partial(): jnp.einsum('bkcgp,bpkd->bkcgd', p_cache.astype(jnp.bfloat16), v_cache, pr...  38.2 us
    reduce_sum x2, other arithmetic, attend_partial(): row_sum = jnp.sum(p_cache, axis=-1) + jnp.sum(p_own, axis=-1)  38.1 us
    pmax x1, blocking collectives, per_device(): glob_max = lax.pmax(row_max, 'cp')  15.6 us
    psum x1, blocking collectives, per_device(): lax.psum((weighted * factor[..., None], row_sum * factor), 'cp')  15.5 us
  transfers between devices with their start and end apart: 2, of which 2 were waited for; matrix products, arithmetic and copies ran while one was open for 0% of the time, Pallas kernels for 0%

commit v1 on v0

v1 whole, which is shorter than its diff:
```python
import functools

import jax
import jax.numpy as jnp
from jax import lax
from jax.experimental import pallas as pl
from jax.experimental.pallas import tpu as pltpu
from jax.sharding import PartitionSpec as P

HEAD_DIM = 128
NEG = -3e38
FLOOR = -1e38
LOG2E = 1.4426950408889634
NBUF = 3
CHUNK = 512


def rms_scale(tensor, norm_gain):
    mean_sq = jnp.mean(jnp.square(tensor), axis=-1, keepdims=True)
    return tensor * lax.rsqrt(mean_sq + 1e-6) * norm_gain


def rope_apply(tensor, positions):
    half_dim = HEAD_DIM // 2
    inv_freq = 1.0 / (1000000.0 ** (jnp.arange(half_dim, dtype=jnp.float32) * 2.0 / HEAD_DIM))
    angles = positions.astype(jnp.float32)[..., None] * inv_freq
    cos_t = jnp.cos(angles)[..., None, :]
    sin_t = jnp.sin(angles)[..., None, :]
    lead_half = tensor[..., :half_dim]
    tail_half = tensor[..., half_dim:]
    return jnp.concatenate([lead_half * cos_t - tail_half * sin_t, tail_half * cos_t + lead_half * sin_t], axis=-1)


def project_new(hidden, attn_norm, w_q, w_k, w_v, q_norm, k_norm, prefix_len):
    n_seq, n_new, d_model = hidden.shape
    kv_count = w_k.shape[1] // HEAD_DIM
    head_count = w_q.shape[1] // HEAD_DIM
    normed = rms_scale(hidden.astype(jnp.float32), attn_norm.astype(jnp.float32)).astype(jnp.bfloat16)
    q_lin = jnp.einsum('bce,ef->bcf', normed, w_q, preferred_element_type=jnp.float32).astype(jnp.bfloat16)
    k_lin = jnp.einsum('bce,ef->bcf', normed, w_k, preferred_element_type=jnp.float32).astype(jnp.bfloat16)
    v_lin = jnp.einsum('bce,ef->bcf', normed, w_v, preferred_element_type=jnp.float32).astype(jnp.bfloat16)
    positions = prefix_len[:, None] + jnp.arange(n_new, dtype=jnp.int32)[None, :]
    q_heads = q_lin.reshape(n_seq, n_new, head_count, HEAD_DIM).astype(jnp.float32)
    k_heads = k_lin.reshape(n_seq, n_new, kv_count, HEAD_DIM).astype(jnp.float32)
    q_rot = rope_apply(rms_scale(q_heads, q_norm.astype(jnp.float32)), positions).astype(jnp.bfloat16)
    k_new = rope_apply(rms_scale(k_heads, k_norm.astype(jnp.float32)), positions).astype(jnp.bfloat16)
    v_new = v_lin.reshape(n_seq, n_new, kv_count, HEAD_DIM)
    return q_rot, k_new, v_new


def head_rows(ref, start, count, head):
    return ref[pl.ds(start * 4 + head, count, stride=4), :]


def pair_rows(ref, start, count, pair):
    return jnp.concatenate([head_rows(ref, start, count, 2 * pair), head_rows(ref, start, count, 2 * pair + 1)], axis=1)


def query_weights(q_ref, b, pair):
    def head(h):
        return jnp.concatenate([q_ref[b, :, (2 * h + g) * 128:(2 * h + g + 1) * 128] for g in range(2)], axis=0)
    zero = jnp.zeros((64, 128), jnp.bfloat16)
    top = jnp.concatenate([head(2 * pair), zero], axis=1)
    low = jnp.concatenate([zero, head(2 * pair + 1)], axis=1)
    return jnp.concatenate([top, low], axis=0).T


def score_pass(q_ref, kn_ref, kbuf, scores, own_scores, b, limit, own):
    tops = []
    row = lax.broadcasted_iota(jnp.int32, (CHUNK, 128), 0)
    own_row = lax.broadcasted_iota(jnp.int32, (32, 128), 0)
    token = lax.broadcasted_iota(jnp.int32, (32, 128), 1) % 32
    for pair in range(2):
        wq = query_weights(q_ref, b, pair)
        top = jnp.full((8, 128), FLOOR, jnp.float32)
        for c in range(2048 // CHUNK):
            s = jnp.dot(pair_rows(kbuf, c * CHUNK, CHUNK, pair), wq, preferred_element_type=jnp.float32)
            s = jnp.where(row < limit - c * CHUNK, s, NEG)
            scores[pair, pl.ds(c * CHUNK, CHUNK), :] = s
            top = jnp.maximum(top, jnp.max(s.reshape(CHUNK // 8, 8, 128), axis=0))
        s = jnp.dot(pair_rows(kn_ref.at[b], 0, 32, pair), wq, preferred_element_type=jnp.float32)
        s = jnp.where(own_row <= token - own, s, NEG)
        own_scores[pair] = s
        top = jnp.maximum(top, jnp.max(s.reshape(4, 8, 128), axis=0))
        tops.append(jnp.max(top, axis=0, keepdims=True))
    return tops


def value_pass(vn_ref, vbuf, scores, own_scores, tops, b):
    scale = HEAD_DIM ** -0.5 * LOG2E
    outs = []
    for pair in range(2):
        top = tops[pair]
        total = jnp.zeros((8, 128), jnp.float32)
        out = jnp.zeros((128, 256), jnp.float32)
        for c in range(2048 // CHUNK):
            p = jnp.exp2((scores[pair, pl.ds(c * CHUNK, CHUNK), :] - top) * scale)
            total = total + jnp.sum(p.reshape(CHUNK // 8, 8, 128), axis=0)
            out = out + jnp.dot(p.astype(jnp.bfloat16).T, pair_rows(vbuf, c * CHUNK, CHUNK, pair), preferred_element_type=jnp.float32)
        p = jnp.exp2((own_scores[pair] - top) * scale)
        total = total + jnp.sum(p.reshape(4, 8, 128), axis=0)
        out = out + jnp.dot(p.astype(jnp.bfloat16).T, pair_rows(vn_ref.at[b], 0, 32, pair), preferred_element_type=jnp.float32)
        outs.append((out, jnp.sum(total, axis=0, keepdims=True)))
    return outs


def stat_tile(rows, lane0):
    lane = lax.broadcasted_iota(jnp.int32, (32, 128), 1)
    tile = jnp.zeros((32, 128), jnp.float32)
    for pair in range(2):
        col = jnp.broadcast_to(rows[pair], (128, 128)).T
        for i in range(4):
            tile = jnp.where(lane == lane0 + 4 * pair + i, col[i * 32:(i + 1) * 32], tile)
    return tile


def attend_kernel(limit_ref, q_ref, kn_ref, vn_ref, k_hbm, v_hbm, w_ref, kbuf, vbuf, scores, own_scores, ksem, vsem):
    n_seq = q_ref.shape[0]

    def copies(b):
        slot = lax.rem(b, NBUF)
        return (pltpu.make_async_copy(k_hbm.at[b], kbuf.at[slot], ksem.at[slot]),
                pltpu.make_async_copy(v_hbm.at[b], vbuf.at[slot], vsem.at[slot]))

    for b in range(NBUF - 1):
        for copy in copies(b):
            copy.start()
    own = limit_ref[n_seq]
    copies(0)[0].wait()
    tops = score_pass(q_ref, kn_ref, kbuf.at[0], scores.at[0], own_scores.at[0], 0, limit_ref[0], own)

    def step(b, tops, last):
        slot = lax.rem(b, NBUF)
        par = lax.rem(b, 2)
        copies(b)[1].wait()
        if not last:
            nxt = lax.rem(b + 1, NBUF)
            copies(b + 1)[0].wait()

            @pl.when(b + NBUF - 1 < n_seq)
            def _():
                for copy in copies(b + NBUF - 1):
                    copy.start()
            new_tops = score_pass(q_ref, kn_ref, kbuf.at[nxt], scores.at[1 - par], own_scores.at[1 - par], b + 1, limit_ref[b + 1], own)
        outs = value_pass(vn_ref, vbuf.at[slot], scores.at[par], own_scores.at[par], tops, b)
        for pair in range(2):
            out = outs[pair][0]
            for i in range(4):
                head = 4 * pair + i
                w_ref[b, :, head * 128:(head + 1) * 128] = out[i * 32:(i + 1) * 32, (i // 2) * 128:(i // 2 + 1) * 128]
        w_ref[b, :, 1024:1152] = stat_tile(tops, 0) + stat_tile([o[1] for o in outs], 8)
        return None if last else tuple(new_tops)

    tops = lax.fori_loop(0, n_seq - 1, lambda b, t: step(b, t, False), tuple(tops))
    step(n_seq - 1, tops, True)


def attend(q, k_new, v_new, k_cache, v_cache, limits):
    n_seq = q.shape[0]
    rows = k_cache.shape[1] * 4
    vmem = pl.BlockSpec(memory_space=pltpu.VMEM)
    return pl.pallas_call(
        attend_kernel,
        out_shape=jax.ShapeDtypeStruct((n_seq, 32, 1152), jnp.float32),
        in_specs=[pl.BlockSpec(memory_space=pltpu.SMEM), vmem, vmem, vmem, pl.BlockSpec(memory_space=pl.ANY), pl.BlockSpec(memory_space=pl.ANY)],
        out_specs=vmem,
        scratch_shapes=[
            pltpu.VMEM((NBUF, rows, 128), jnp.bfloat16),
            pltpu.VMEM((NBUF, rows, 128), jnp.bfloat16),
            pltpu.VMEM((2, 2, 2048, 128), jnp.float32),
            pltpu.VMEM((2, 2, 32, 128), jnp.float32),
            pltpu.SemaphoreType.DMA((NBUF,)),
            pltpu.SemaphoreType.DMA((NBUF,)),
        ],
        compiler_params=pltpu.CompilerParams(vmem_limit_bytes=48 * 1024 * 1024),
        cost_estimate=pl.CostEstimate(flops=17_000_000_000, bytes_accessed=140_000_000, transcendentals=17_000_000),
    )(limits, q, k_new.reshape(n_seq, 128, 128), v_new.reshape(n_seq, 128, 128), k_cache.reshape(n_seq, rows, 128), v_cache.reshape(n_seq, rows, 128))


def solution(mesh):
    def per_device(hidden, prefix_len, k_cache, v_cache, attn_norm, w_q, w_k, w_v, w_o, q_norm, k_norm):
        n_seq, n_new, d_model = hidden.shape
        cp = lax.axis_index('cp')
        tp = lax.axis_index('tp')
        q_rot, k_new, v_new = project_new(hidden, attn_norm, w_q, w_k, w_v, q_norm, k_norm, prefix_len)
        limits = jnp.concatenate([prefix_len - cp * 2048, jnp.where(cp == 3, 0, 64)[None]]).astype(jnp.int32)
        w = attend(q_rot.reshape(n_seq, n_new, 1024), k_new, v_new, k_cache, v_cache, limits)

        def swap(array, axis, bit):
            count = mesh.shape[axis]
            return lax.ppermute(array, axis, [(i, i ^ bit) for i in range(count)])

        def keep_send(array, which):
            half = array.shape[1] // 2
            first, second = array[:, :half], array[:, half:]
            return jnp.where(which == 0, first, second), jnp.where(which == 0, second, first)

        def merge(a, b):
            ma, mb = a[..., 1024:1032], b[..., 1024:1032]
            m = jnp.maximum(ma, mb)
            scale = HEAD_DIM ** -0.5 * LOG2E
            fa, fb = jnp.exp2((ma - m) * scale), jnp.exp2((mb - m) * scale)
            shape = a.shape[:2] + (8, 128)
            w = a[..., :1024].reshape(shape) * fa[..., None] + b[..., :1024].reshape(shape) * fb[..., None]
            l = a[..., 1032:1040] * fa + b[..., 1032:1040] * fb
            return w, m, l

        def pack(w, m, l):
            rest = jnp.zeros(m.shape[:2] + (112,), jnp.float32)
            return jnp.concatenate([w.reshape(w.shape[:2] + (1024,)), m, l, rest], axis=-1)

        keep, send = keep_send(w, cp % 2)
        half = pack(*merge(keep, swap(send, 'cp', 1)))
        keep, send = keep_send(half, cp // 2)
        w4, _, l4 = merge(keep, swap(send, 'cp', 2))
        o = (w4 / l4[..., None]).astype(jnp.bfloat16).reshape(n_seq * 8, 1024)
        part = jnp.dot(o, w_o, preferred_element_type=jnp.float32)
        first, second = part[:, :1024], part[:, 1024:]
        mine = jnp.where(tp == 0, first, second) + swap(jnp.where(tp == 0, second, first), 'tp', 1)
        ay = swap(mine, 'tp', 1)
        ax = swap(mine, 'cp', 2)
        dh = mine.shape[0] // 2
        d0 = swap(ay[:dh], 'cp', 2)
        d1 = swap(ax[dh:], 'tp', 1)
        diag = jnp.concatenate([d0, d1], axis=0)
        x_mine = jnp.concatenate([jnp.where(tp == 0, mine, ay), jnp.where(tp == 0, ay, mine)], axis=1)
        x_other = jnp.concatenate([jnp.where(tp == 0, ax, diag), jnp.where(tp == 0, diag, ax)], axis=1)
        x_mine = x_mine.reshape(n_seq, 8, d_model)
        x_other = x_other.reshape(n_seq, 8, d_model)
        x = cp // 2
        core = jnp.concatenate([jnp.where(x == 0, x_mine, x_other), jnp.where(x == 0, x_other, x_mine)], axis=1)
        peer = swap(core, 'cp', 1)
        k = cp % 2
        total = jnp.concatenate([jnp.where(k == 0, core, peer), jnp.where(k == 0, peer, core)], axis=1)
        block_out = (hidden.astype(jnp.float32) + total).astype(jnp.bfloat16)
        return block_out, k_new, v_new

    cache_spec = P('dp', 'cp', 'tp', None)
    arg_specs = (P('dp', None, None), P('dp'), cache_spec, cache_spec, P(None), P(None, 'tp'), P(None, 'tp'), P(None, 'tp'), P('tp', None), P(None), P(None))
    out_specs = (P('dp', None, None), P('dp', None, 'tp', None), P('dp', None, 'tp', None))
    return jax.shard_map(per_device, mesh=mesh, in_specs=arg_specs, out_specs=out_specs, check_vma=False)
```

time: 513 us -> 255 us (0.50)
  waiting for transfers between devices: 255 us -> 84.8 us
  matrix products: 132 us -> 21.7 us
  Pallas kernels: 0 us -> 60.9 us
  blocking collectives: 31.2 us -> 0 us
  other arithmetic: 63.7 us -> 49.8 us
  between operations: 14.5 us -> 0.99 us
  local copies, waits for them, and re-layouts: 11.8 us -> 24.8 us
  starting transfers between devices: 0.08 us -> 11.2 us
    psum x2 -> x0, waiting for transfers between devices: 255 us -> none  [the longest x1 190 us: per_device(): out_proj = lax.psum(out_partial(attn_out, w_o), 'tp')]
    dot_general x5 -> x1, matrix products: 116 us -> 4.02 us  [per_device(): part = jnp.dot(o, w_o, preferred_element_type=jnp.float32)]
    ppermute x0 -> x8, waiting for transfers between devices: none -> 84.8 us  [swap(): return lax.ppermute(array, axis, [(i, i ^ bit) for i in range(count)])]
    pallas_call x0 -> x1, Pallas kernels: none -> 60.9 us  [attend(): pl.pallas_call(attend_kernel, out_shape=jax.ShapeDtypeStruct((n_seq, 32,...]
    reduce_sum x2 -> x0, other arithmetic: 38.1 us -> none  [attend_partial(): row_sum = jnp.sum(p_cache, axis=-1) + jnp.sum(p_own, axis=-1)]
    pmax x1 -> x0, blocking collectives: 15.6 us -> none  [per_device(): glob_max = lax.pmax(row_max, 'cp')]
    psum x1 -> x0, blocking collectives: 15.5 us -> none  [per_device(): lax.psum((weighted * factor[..., None], row_sum * factor), 'cp')]
    ppermute x0 -> x8, starting transfers between devices: none -> 11.2 us  [swap(): return lax.ppermute(array, axis, [(i, i ^ bit) for i in range(count)])]
  transfers between devices with their start and end apart: 2 -> 8, of which waited for: 2 -> 7; matrix products, arithmetic and copies ran while one was open for 0% -> 2% of each run, Pallas kernels for 0% -> 0%
where the time goes in v1:
time: 255 us; the launch traced here: 254 us
  waiting for transfers between devices  84.8 us (33%)
  Pallas kernels  60.9 us (24%)
  other arithmetic  49.8 us (20%)
  local copies, waits for them, and re-layouts  24.8 us (10%)
  matrix products  21.7 us (9%)
  starting transfers between devices  11.2 us (4%)
    ppermute x8, waiting for transfers between devices, swap(): return lax.ppermute(array, axis, [(i, i ^ bit) for i in range(count)])  84.8 us
    pallas_call x1, Pallas kernels, attend(): pl.pallas_call(attend_kernel, out_shape=jax.ShapeDtypeStruct((n_seq, 32,...  60.9 us
    ppermute x8, starting transfers between devices, swap(): return lax.ppermute(array, axis, [(i, i ^ bit) for i in range(count)])  11.2 us
    concatenate x3, other arithmetic, rope_apply(): jnp.concatenate([lead_half * cos_t - tail_half * sin_t, tail_half * cos_t...  8.35 us
    dot_general x1, matrix products, project_new(): jnp.einsum('bce,ef->bcf', normed, w_q, preferred_element_type=jnp.float32)  7.61 us
    dot_general x1, matrix products, project_new(): jnp.einsum('bce,ef->bcf', normed, w_k, preferred_element_type=jnp.float32)  6.57 us
    reduce_sum x3, other arithmetic, rms_scale(): mean_sq = jnp.mean(jnp.square(tensor), axis=-1, keepdims=True)  6.17 us
    select_n x2, other arithmetic, keep_send(): jnp.where(which == 0, first, second)  5.27 us
  transfers between devices with their start and end apart: 8, of which 7 were waited for; matrix products, arithmetic and copies ran while one was open for 2% of the time, Pallas kernels for 0%

profile of v1, /device:TPU:0, one launch (start us, length us, event | category | flops | bytes accessed | tf_op | source)
XLA Modules:
  0.0 254.1 jit_solution(3144173270567517688)
XLA Ops:
  1.6 1.1 broadcast_subtract_fusion
  4.7 3.1 %fusion = f32[32,32]{1,0:T(8,128)S(1)} fusion(bf16[32,32,2048]{2,1,0:T(8,128)(2,1)} %param.11), kind=kLoop, calls=%fused_computation.3 | loop fusion | flops 6290432 | bytes 4198400 | tf_op jit(solution)/shard_map/reduce_sum | solution.py:19
  7.8 3.5 %fusion.30 = bf16[32,32,512]{2,1,0:T(8,128)(2,1)} fusion(bf16[2048,512]{1,0:T(8,128)(2,1)S(1)} %copy-done, bf16[32,32,2048]{2,1,0:T(8,128)(2,1)S(1)} %copy-done.4, f32[2048]{0:T(1024)S(1)} %convert_element_type.60, f32[32,32]{1,0:T(8,128)S(1)} %add_rsqrt_fusion.2), kind=kOutput, calls=%fused_computation.39 | convolution fusion | flops 2156396544 | bytes 7352320 | tf_op jit(solution)/shard_map/bce,ef->bcf/dot_general | solution.py:41
  11.3 1.7 reshape_reshape.3.vn_ref
  13.0 6.6 %fusion.25 = f32[32,32,512]{2,1,0:T(8,128)} fusion(bf16[2048,512]{1,0:T(8,128)(2,1)} %param.17, bf16[32,32,2048]{2,1,0:T(8,128)(2,1)} %param.11, f32[2048]{0:T(1024)S(1)} %convert_element_type.60, f32[32,32]{1,0:T(8,128)S(1)} %add_rsqrt_fusion.2), kind=kOutput, calls=%fused_computation.38 | convolution fusion | flops 2156920832 | bytes 8400896 | tf_op jit(solution)/shard_map/bce,ef->bcf/dot_general | solution.py:40
  19.5 1.9 reshape.121
  21.5 2.0 multiply_reduce_fusion
  23.4 1.3 copy.21
  24.8 1.1 copy.22
  25.9 7.6 %convert_convert_fusion = f32[32,32,1024]{2,1,0:T(8,128)S(1)} fusion(bf16[2048,1024]{1,0:T(8,128)(2,1)} %param.16, bf16[32,32,2048]{2,1,0:T(8,128)(2,1)} %param.11, f32[2048]{0:T(1024)S(1)} %convert_element_type.60, f32[32,32]{1,0:T(8,128)S(1)} %add_rsqrt_fusion.2), kind=kOutput, calls=%fused_computation.34 | convolution fusion | flops 4305453056 | bytes 12595200 | tf_op jit(solution)/shard_map/bce,ef->bcf/dot_general | solution.py:39
  33.5 1.0 copy.26
  34.5 1.1 fusion.4
  35.7 1.9 multiply_cosine_fusion
  37.6 1.4 multiply_multiply_fusion
  39.0 2.8 %subtract_convert_fusion.1 = (bf16[32,32,4,64]{3,2,1,0:T(4,128)(2,1)}, bf16[32,32,4,64]{3,2,1,0:T(4,128)(2,1)}) fusion(f32[32,32,4,128]{3,2,1,0:T(4,128)S(1)} %multiply_multiply_fusion, f32[32,32,64]{2,1,0:T(8,128)S(1)} %get-tuple-element.27, f32[32,32,64]{2,1,0:T(8,128)S(1)} %get-tuple-element.26), kind=kLoop, calls=%fused_computation.31 | loop fusion | flops 2097152 | bytes 3670016 | tf_op jit(solution)/shard_map/convert.7
  41.8 1.2 fusion.5
  43.1 1.8 subtract_convert_fusion
  44.8 2.5 pad_maximum_fusion.1
  47.3 2.8 %convert_element_type.67.q_ref = bf16[32,32,1024]{2,1,0:T(8,128)(2,1)S(1)} reshape(bf16[32,32,8,128]{3,2,1,0:T(8,128)(2,1)} %pad_maximum_fusion.1) | data formatting | bytes 4194304 | tf_op jit(solution)/shard_map/convert_element_type | solution.py:45
  50.2 2.1 pad_maximum_fusion.4.kn_ref
  52.4 60.9 %shard_map.130 = f32[32,32,1152]{2,1,0:T(8,128)} custom-call(s32[33]{0:T(128)S(1)} %pad_add_fusion.limit_ref, bf16[32,32,1024]{2,1,0:T(8,128)(2,1)S(1)} %convert_element_type.67.q_ref, bf16[32,128,128]{2,1,0:T(8,128)(2,1)S(1)} %pad_maximum_fusion.4.kn_ref, bf16[32,128,128]{2,1,0:T(8,128)(2,1)S(1)} %reshape_reshape.3.vn_ref, ...), custom_call_target="tpu_custom_call" | custom-call | flops 16999999488 | bytes 140000000 | tf_op jit(solution)/shard_map/pallas_call | solution.py:162
  113.3 4.1 %slice_select_fusion.1 = (f32[32,16,1152]{2,1,0:T(8,128)S(1)}, f32[32,16,1152]{2,1,0:T(8,128)}) fusion(f32[32,32,1152]{2,1,0:T(8,128)} %shard_map.130, pred[]{:T(512)S(6)} %eq.11), kind=kLoop, calls=%fused_computation.17 | loop fusion | flops 1179648 | bytes 9437185 | tf_op jit(solution)/shard_map/jit(_where)/select_n | solution.py:196
  118.2 4.2 %collective-permute-done = f32[32,16,1152]{2,1,0:T(8,128)} collective-permute-done((f32[32,16,1152]{2,1,0:T(8,128)}, f32[32,16,1152]{2,1,0:T(8,128)}, u32[]{:S(2)}, u32[]{:S(2)}) %collective-permute-start) | collective-permute-done | bytes 2359328 | tf_op jit(solution)/shard_map/ppermute | solution.py:191
  122.4 1.3 fusion.45
  123.7 1.9 mul.225
  125.6 2.8 %mul.226 = f32[32,16,1024]{2,1,0:T(8,128)} reshape(f32[32,16,8,128]{3,2,1,0:T(8,128)} %mul.225) | data formatting | bytes 4194304 | tf_op jit(solution)/shard_map/mul | solution.py:204
  128.3 1.9 mul.228
  130.3 2.7 %mul.229 = f32[32,16,1024]{2,1,0:T(8,128)} reshape(f32[32,16,8,128]{3,2,1,0:T(8,128)} %mul.228) | data formatting | bytes 4194304 | tf_op jit(solution)/shard_map/mul | solution.py:204
  133.0 5.1 %fusion.13 = f32[32,16,1024]{2,1,0:T(8,128)} fusion(f32[32,16,1024]{2,1,0:T(8,128)} %mul.229, f32[32,16,1152]{2,1,0:T(8,128)} %collective-permute-done, f32[32,16,1024]{2,1,0:T(8,128)} %mul.226, f32[32,16,1152]{2,1,0:T(8,128)S(1)} %get-tuple-element.14), kind=kLoop, calls=%fused_computation.21 | loop fusion | flops 1572864 | bytes 10485760 | tf_op jit(solution)/shard_map/add | solution.py:204
  138.2 2.9 %concatenate.42 = f32[32,16,1152]{2,1,0:T(8,128)S(1)} concatenate(f32[32,16,1024]{2,1,0:T(8,128)} %fusion.13, f32[32,16,8]{2,1,0:T(8,128)S(1)} %get-tuple-element.9, f32[32,16,8]{2,1,0:T(8,128)S(1)} %get-tuple-element.6, f32[32,16,112]{2,1,0:T(8,128)S(1)} %broadcast_in_dim.5), dimensions={2} | concatenate | bytes 4718592 | tf_op jit(solution)/shard_map/concatenate | solution.py:210
  141.0 1.2 slice_select_fusion.3
  142.2 2.8 %collective-permute-start.1 = (f32[32,8,1152]{2,1,0:T(8,128)}, f32[32,8,1152]{2,1,0:T(8,128)S(1)}, u32[]{:S(2)}, u32[]{:S(2)}) collective-permute-start(f32[32,8,1152]{2,1,0:T(8,128)} %get-tuple-element.21), channel_id=1, source_target_pairs={{0,2},{1,3},{2,0},{3,1},{4,6},{5,7},{6,4},{7,5}} | collective-permute-start | bytes 3538952 | tf_op jit(solution)/shard_map/ppermute | solution.py:191
  145.0 26.3 %collective-permute-done.1 = f32[32,8,1152]{2,1,0:T(8,128)S(1)} collective-permute-done((f32[32,8,1152]{2,1,0:T(8,128)}, f32[32,8,1152]{2,1,0:T(8,128)S(1)}, u32[]{:S(2)}, u32[]{:S(2)}) %collective-permute-start.1) | collective-permute-done | bytes 1179680 | tf_op jit(solution)/shard_map/ppermute | solution.py:191
  171.8 4.0 %fusion.40 = f32[256,2048]{1,0:T(8,128)S(1)} fusion(bf16[1024,2048]{1,0:T(8,128)(2,1)} %param.19, f32[32,8,1152]{2,1,0:T(8,128)S(1)} %collective-permute-done.1, f32[32,8,1152]{2,1,0:T(8,128)S(1)} %get-tuple-element.20, f32[32,8,8]{1,2,0:T(8,128)S(1)} %copy.25, f32[32,8,8]{1,2,0:T(8,128)S(1)} %copy.24, f32[32,8,8]{1,2,0:T(8,128)S(1)} %copy.23), kind=kOutput, calls=%fused_computation.55 | convolution fusion | flops 1075052544 | bytes 8781824 | tf_op jit(solution)/shard_map/dot_general | solution.py:217
  175.9 1.8 collective-permute-start.2
  177.7 22.9 %collective-permute-done.2 = f32[256,1024]{1,0:T(8,128)S(1)} collective-permute-done((f32[256,1024]{1,0:T(8,128)S(1)}, f32[256,1024]{1,0:T(8,128)S(1)}, u32[]{:S(2)}, u32[]{:S(2)}) %collective-permute-start.2) | collective-permute-done | bytes 1048608 | tf_op jit(solution)/shard_map/ppermute | solution.py:191
  200.9 1.5 collective-permute-start.3
  202.4 1.5 collective-permute-start.4
  203.9 20.8 %collective-permute-done.3 = f32[256,1024]{1,0:T(8,128)S(1)} collective-permute-done((f32[256,1024]{1,0:T(8,128)S(1)}, f32[256,1024]{1,0:T(8,128)S(1)}, u32[]{:S(2)}, u32[]{:S(2)}) %collective-permute-start.3) | collective-permute-done | bytes 1048608 | tf_op jit(solution)/shard_map/ppermute | solution.py:191
  224.8 1.2 collective-permute-start.5
  226.1 1.5 collective-permute-start.6
  227.8 9.1 %collective-permute-done.5 = f32[128,1024]{1,0:T(8,128)S(1)} collective-permute-done((f32[128,1024]{1,0:T(8,128)S(1)}, f32[128,1024]{1,0:T(8,128)S(1)}, u32[]{:S(2)}, u32[]{:S(2)}) %collective-permute-start.5) | collective-permute-done | bytes 524320 | tf_op jit(solution)/shard_map/ppermute | solution.py:191
  237.9 2.7 %pad_maximum_fusion = f32[32,16,2048]{2,1,0:T(8,128)} fusion(f32[32,8,2048]{2,1,0:T(8,128)S(1)} %get-tuple-element.17, f32[32,8,2048]{2,1,0:T(8,128)S(1)} %get-tuple-element.16), kind=kLoop, calls=%fused_computation.11 | loop fusion | flops 1048576 | bytes 8388608 | tf_op jit(solution)/shard_map/concatenate | solution.py:231
  240.6 2.2 reshape.119
  242.8 3.8 %pad_maximum_fusion.5 = bf16[32,32,4,128]{3,2,1,0:T(4,128)(2,1)} fusion(bf16[32,32,4,64]{3,2,1,0:T(4,128)(2,1)} %get-tuple-element.19, bf16[32,32,4,64]{3,2,1,0:T(4,128)(2,1)S(1)} %copy-done.6), kind=kLoop, calls=%fused_computation.49 | loop fusion | flops 2097152 | bytes 2097152 | tf_op jit(solution)/shard_map/concatenate | solution.py:31
  246.6 1.1 collective-permute-done.7
  247.7 3.5 %broadcast_select_fusion.1 = (f32[32,16,2048]{2,1,0:T(8,128)S(1)}, f32[32,16,2048]{2,1,0:T(8,128)S(1)}) fusion(f32[32,16,2048]{2,1,0:T(8,128)} %collective-permute-done.7, pred[]{:T(512)S(6)} %eq.11, f32[32,8,2048]{2,1,0:T(8,128)S(1)} %copy-done.3, f32[32,8,2048]{2,1,0:T(8,128)S(1)} %get-tuple-element.16), kind=kLoop, calls=%fused_computation.36 | loop fusion | flops 3145728 | bytes 16777216 | tf_op jit(solution)/shard_map/jit(_where)/select_n | solution.py:234
  251.3 2.8 %fusion.3 = bf16[32,32,2048]{2,1,0:T(8,128)(2,1)} fusion(bf16[32,32,2048]{2,1,0:T(8,128)(2,1)S(1)} %copy-done.5, f32[32,16,2048]{2,1,0:T(8,128)S(1)} %get-tuple-element.11, f32[32,16,2048]{2,1,0:T(8,128)S(1)} %get-tuple-element.10), kind=kLoop, calls=%fused_computation.6 | loop fusion | flops 8388608 | bytes 16777216 | tf_op jit(solution)/shard_map/convert_element_type | solution.py:235
  (43 shorter events, 6.0 us)
Async XLA Ops:
  0.6 7.1 %copy-start = (bf16[2048,512]{1,0:T(8,128)(2,1)S(1)}, bf16[2048,512]{1,0:T(8,128)(2,1)}, u32[]{:S(2)}) copy-start(bf16[2048,512]{1,0:T(8,128)(2,1)} %param.18) | copy-start | bytes 6291460
  0.7 7.1 %copy-start.4 = (bf16[32,32,2048]{2,1,0:T(8,128)(2,1)S(1)}, bf16[32,32,2048]{2,1,0:T(8,128)(2,1)}, u32[]{:S(2)}) copy-start(bf16[32,32,2048]{2,1,0:T(8,128)(2,1)} %param.11) | copy-start | bytes 12582916
  34.5 3.1 %copy-start.7 = (f32[32,32,4]{2,1,0:T(8,128)S(1)}, f32[32,32,4]{2,1,0:T(8,128)}, u32[]{:S(2)}) copy-start(f32[32,32,4]{2,1,0:T(8,128)} %copy.22) | copy-start | bytes 49156
  117.4 5.0 %collective-permute-start = (f32[32,16,1152]{2,1,0:T(8,128)}, f32[32,16,1152]{2,1,0:T(8,128)}, u32[]{:S(2)}, u32[]{:S(2)}) collective-permute-start(f32[32,16,1152]{2,1,0:T(8,128)} %get-tuple-element.15), channel_id=1, source_target_pairs={{0,1},{1,0},{2,3},{3,2},{4,5},{5,4},{6,7},{7,6}} | collective-permute-start | bytes 7077896 | tf_op jit(solution)/shard_map/ppermute | solution.py:191
  142.2 29.1 %collective-permute-start.1 = (f32[32,8,1152]{2,1,0:T(8,128)}, f32[32,8,1152]{2,1,0:T(8,128)S(1)}, u32[]{:S(2)}, u32[]{:S(2)}) collective-permute-start(f32[32,8,1152]{2,1,0:T(8,128)} %get-tuple-element.21), channel_id=1, source_target_pairs={{0,2},{1,3},{2,0},{3,1},{4,6},{5,7},{6,4},{7,5}} | collective-permute-start | bytes 3538952 | tf_op jit(solution)/shard_map/ppermute | solution.py:191
  175.9 24.7 %collective-permute-start.2 = (f32[256,1024]{1,0:T(8,128)S(1)}, f32[256,1024]{1,0:T(8,128)S(1)}, u32[]{:S(2)}, u32[]{:S(2)}) collective-permute-start(f32[256,1024]{1,0:T(8,128)S(1)} %slice_select_fusion.4), channel_id=1, source_target_pairs={{0,4},{4,0},{1,5},{5,1},{2,6},{6,2},{3,7},{7,3}} | collective-permute-start | bytes 3145736 | tf_op jit(solution)/shard_map/ppermute | solution.py:191
  200.9 23.9 %collective-permute-start.3 = (f32[256,1024]{1,0:T(8,128)S(1)}, f32[256,1024]{1,0:T(8,128)S(1)}, u32[]{:S(2)}, u32[]{:S(2)}) collective-permute-start(f32[256,1024]{1,0:T(8,128)S(1)} %select_add_fusion), channel_id=1, source_target_pairs={{0,4},{4,0},{1,5},{5,1},{2,6},{6,2},{3,7},{7,3}} | collective-permute-start | bytes 3145736 | tf_op jit(solution)/shard_map/ppermute | solution.py:191
  202.4 23.6 %collective-permute-start.4 = (f32[256,1024]{1,0:T(8,128)S(1)}, f32[256,1024]{1,0:T(8,128)S(1)}, u32[]{:S(2)}, u32[]{:S(2)}) collective-permute-start(f32[256,1024]{1,0:T(8,128)S(1)} %select_add_fusion), channel_id=1, source_target_pairs={{0,2},{1,3},{2,0},{3,1},{4,6},{5,7},{6,4},{7,5}} | collective-permute-start | bytes 3145736 | tf_op jit(solution)/shard_map/ppermute | solution.py:191
  224.8 12.1 %collective-permute-start.5 = (f32[128,1024]{1,0:T(8,128)S(1)}, f32[128,1024]{1,0:T(8,128)S(1)}, u32[]{:S(2)}, u32[]{:S(2)}) collective-permute-start(f32[128,1024]{1,0:T(8,128)S(1)} %slice.118), channel_id=1, source_target_pairs={{0,2},{1,3},{2,0},{3,1},{4,6},{5,7},{6,4},{7,5}} | collective-permute-start | bytes 1572872 | tf_op jit(solution)/shard_map/ppermute | solution.py:191
  226.1 11.2 %collective-permute-start.6 = (f32[128,1024]{1,0:T(8,128)S(1)}, f32[128,1024]{1,0:T(8,128)S(1)}, u32[]{:S(2)}, u32[]{:S(2)}) collective-permute-start(f32[128,1024]{1,0:T(8,128)S(1)} %slice.119), channel_id=1, source_target_pairs={{0,4},{4,0},{1,5},{5,1},{2,6},{6,2},{3,7},{7,3}} | collective-permute-start | bytes 1572872 | tf_op jit(solution)/shard_map/ppermute | solution.py:191
  237.9 2.7 %copy-start.2 = (f32[32,8,2048]{2,1,0:T(8,128)}, f32[32,8,2048]{2,1,0:T(8,128)S(1)}, u32[]{:S(2)}) copy-start(f32[32,8,2048]{2,1,0:T(8,128)S(1)} %get-tuple-element.17) | copy-start | bytes 6291460
  240.6 2.2 copy-start.6
  240.6 7.1 %collective-permute-start.7 = (f32[32,16,2048]{2,1,0:T(8,128)}, f32[32,16,2048]{2,1,0:T(8,128)}, u32[]{:S(2)}, u32[]{:S(2)}) collective-permute-start(f32[32,16,2048]{2,1,0:T(8,128)} %pad_maximum_fusion), channel_id=1, source_target_pairs={{0,1},{1,0},{2,3},{3,2},{4,5},{5,4},{6,7},{7,6}} | collective-permute-start | bytes 12582920 | tf_op jit(solution)/shard_map/ppermute | solution.py:191
  242.8 4.9 %copy-start.3 = (f32[32,8,2048]{2,1,0:T(8,128)S(1)}, f32[32,8,2048]{2,1,0:T(8,128)}, u32[]{:S(2)}) copy-start(f32[32,8,2048]{2,1,0:T(8,128)} %copy-done.2) | copy-start | bytes 6291460
  247.7 3.6 %copy-start.5 = (bf16[32,32,2048]{2,1,0:T(8,128)(2,1)S(1)}, bf16[32,32,2048]{2,1,0:T(8,128)(2,1)}, u32[]{:S(2)}) copy-start(bf16[32,32,2048]{2,1,0:T(8,128)(2,1)} %param.11) | copy-start | bytes 12582916
  251.3 2.8 %copy-start.1 = (bf16[2048,512]{1,0:T(8,128)(2,1)S(1)}, bf16[2048,512]{1,0:T(8,128)(2,1)}, u32[]{:S(2)}) copy-start(bf16[2048,512]{1,0:T(8,128)(2,1)} %param.18) | copy-start | bytes 6291460

commit v2 on v1

--- a/solution.py
+++ b/solution.py
@@ -114,125 +114,264 @@
     return tile
 
 
-def attend_kernel(limit_ref, q_ref, kn_ref, vn_ref, k_hbm, v_hbm, w_ref, kbuf, vbuf, scores, own_scores, ksem, vsem):
-    n_seq = q_ref.shape[0]
+N_SEQ = 32
+BATCH = 4
+N_BATCH = N_SEQ // BATCH
+LAG_X, LAG_Y, LAG_G, LAG_D, LAG_F = 6, 9, 13, 16, 18
+SCALE = HEAD_DIM ** -0.5 * LOG2E
+MESH = pl.DeviceIdType.MESH
+
+
+def merge_parts(a, r):
+    sa, sr = a[:, 1024:], r[:, 1024:]
+    lane = lax.broadcasted_iota(jnp.int32, sa.shape, 1)
+    top = jnp.maximum(sa, sr)
+    fa = jnp.where(lane < 8, jnp.exp2((sa - top) * SCALE), 0.0)
+    fr = jnp.where(lane < 8, jnp.exp2((sr - top) * SCALE), 0.0)
+    total = sa * pltpu.roll(fa, 8, 1) + sr * pltpu.roll(fr, 8, 1)
+    parts = []
+    for h in range(8):
+        cols = slice(h * 128, (h + 1) * 128)
+        parts.append(a[:, cols] * fa[:, h:h + 1] + r[:, cols] * fr[:, h:h + 1])
+    return parts, jnp.where(lane < 8, top, total)
+
+
+def block_kernel(limit_ref, q_ref, kn_ref, vn_ref, x_ref, wo_ref, k_hbm, v_hbm, out_ref,
+                 kbuf, vbuf, scores, own_scores, tops_ref, part, part_in, half, half_in, proj, proj_in, gath,
+                 ksem, vsem, d_send, d_recv, x_send, x_recv, y_send, y_recv, gx_send, gx_recv, gy_send, gy_recv,
+                 dx_send, dx_recv, dy_send, dy_recv, c_send, c_recv):
+    dp, tp, cp = lax.axis_index('dp'), lax.axis_index('tp'), lax.axis_index('cp')
+    x, k = cp // 2, cp % 2
+    core_peer = (dp, tp, cp + 1 - 2 * k)
+    x_peer = (dp, tp, cp + 2 - 4 * x)
+    y_peer = (dp, 1 - tp, cp)
+
+    barrier = pltpu.get_barrier_semaphore()
+    for peer in (core_peer, x_peer, y_peer):
+        pl.semaphore_signal(barrier, inc=1, device_id=peer, device_id_type=MESH)
 
     def copies(b):
         slot = lax.rem(b, NBUF)
         return (pltpu.make_async_copy(k_hbm.at[b], kbuf.at[slot], ksem.at[slot]),
                 pltpu.make_async_copy(v_hbm.at[b], vbuf.at[slot], vsem.at[slot]))
 
+    def remote(src, dst, send, recv, peer):
+        return pltpu.make_async_remote_copy(src_ref=src, dst_ref=dst, send_sem=send, recv_sem=recv, device_id=peer, device_id_type=MESH)
+
+    def core_copy(b):
+        return remote(part.at[b, pl.ds(pl.multiple_of((1 - k) * 16, 16), 16)], part_in.at[b], d_send.at[b], d_recv.at[b], core_peer)
+
+    def x_copy(b):
+        return remote(half.at[b, pl.ds(pl.multiple_of((1 - x) * 8, 8), 8)], half_in.at[b], x_send.at[b], x_recv.at[b], x_peer)
+
+    def y_copy(n):
+        return remote(proj.at[n, 1 - tp], proj_in.at[n], y_send.at[n], y_recv.at[n], y_peer)
+
+    def slot_of(xx, yy, kk):
+        return (xx * 2 + yy) * 2 + kk
+
+    mine = slot_of(x, tp, k)
+    from_x = slot_of(1 - x, tp, k)
+    from_y = slot_of(x, 1 - tp, k)
+    diag = slot_of(1 - x, 1 - tp, k)
+
+    def gx_copy(n):
+        return remote(gath.at[mine, n], gath.at[mine, n], gx_send.at[n], gx_recv.at[n], x_peer)
+
+    def gy_copy(n):
+        return remote(gath.at[mine, n], gath.at[mine, n], gy_send.at[n], gy_recv.at[n], y_peer)
+
+    def dx_copy(n):
+        return remote(gath.at[from_y, n, pl.ds(0, 16)], gath.at[from_y, n, pl.ds(0, 16)], dx_send.at[n], dx_recv.at[n], x_peer)
+
+    def dy_copy(n):
+        return remote(gath.at[from_x, n, pl.ds(16, 16)], gath.at[from_x, n, pl.ds(16, 16)], dy_send.at[n], dy_recv.at[n], y_peer)
+
+    def c_copy(n, slot, i):
+        return remote(gath.at[slot, n], gath.at[slot, n], c_send.at[i, n], c_recv.at[i, n], core_peer)
+
     for b in range(NBUF - 1):
         for copy in copies(b):
             copy.start()
-    own = limit_ref[n_seq]
+    own = limit_ref[N_SEQ]
+
+    def run_scores(b, par):
+        tops = score_pass(q_ref, kn_ref, kbuf.at[lax.rem(b, NBUF)], scores.at[par], own_scores.at[par], b, limit_ref[b], own)
+        for pair in range(2):
+            tops_ref[par, pair] = jnp.broadcast_to(tops[pair], (8, 128))
+
     copies(0)[0].wait()
-    tops = score_pass(q_ref, kn_ref, kbuf.at[0], scores.at[0], own_scores.at[0], 0, limit_ref[0], own)
-
-    def step(b, tops, last):
-        slot = lax.rem(b, NBUF)
-        par = lax.rem(b, 2)
-        copies(b)[1].wait()
-        if not last:
-            nxt = lax.rem(b + 1, NBUF)
-            copies(b + 1)[0].wait()
-
-            @pl.when(b + NBUF - 1 < n_seq)
+    run_scores(0, 0)
+    pl.semaphore_wait(barrier, 3)
+
+    def step(it, carry):
+        @pl.when(it < N_SEQ)
+        def _():
+            b, par = it, lax.rem(it, 2)
+            copies(b)[1].wait()
+
+            @pl.when(b + 1 < N_SEQ)
+            def _():
+                copies(b + 1)[0].wait()
+
+            @pl.when(b + NBUF - 1 < N_SEQ)
             def _():
                 for copy in copies(b + NBUF - 1):
                     copy.start()
-            new_tops = score_pass(q_ref, kn_ref, kbuf.at[nxt], scores.at[1 - par], own_scores.at[1 - par], b + 1, limit_ref[b + 1], own)
-        outs = value_pass(vn_ref, vbuf.at[slot], scores.at[par], own_scores.at[par], tops, b)
-        for pair in range(2):
-            out = outs[pair][0]
+
+            run_scores(jnp.minimum(b + 1, N_SEQ - 1), 1 - par)
+            tops = [tops_ref[par, pair, 0:1, :] for pair in range(2)]
+            outs = value_pass(vn_ref, vbuf.at[lax.rem(b, NBUF)], scores.at[par], own_scores.at[par], tops, b)
+            for pair in range(2):
+                out = outs[pair][0]
+                for i in range(4):
+                    head = 4 * pair + i
+                    part[b, :, head * 128:(head + 1) * 128] = out[i * 32:(i + 1) * 32, (i // 2) * 128:(i // 2 + 1) * 128]
+            part[b, :, 1024:1152] = stat_tile(tops, 0) + stat_tile([o[1] for o in outs], 8)
+            core_copy(b).start()
+
+        @pl.when((it >= 1) & (it < N_SEQ + 1))
+        def _():
+            b = it - 1
+            core_copy(b).wait_recv()
+            parts, stats = merge_parts(part[b, pl.ds(pl.multiple_of(k * 16, 16), 16), :], part_in[b])
+            for h in range(8):
+                half[b, :, h * 128:(h + 1) * 128] = parts[h]
+            half[b, :, 1024:] = stats
+            x_copy(b).start()
+
+        def batch_of(lag):
+            n = (it - lag) // BATCH
+            return n, (it >= lag) & ((it - lag) % BATCH == 0) & (n < N_BATCH)
+
+        n_x, now_x = batch_of(LAG_X)
+
+        @pl.when(now_x)
+        def _():
+            n = n_x
+            for i in range(BATCH):
+                x_copy(n * BATCH + i).wait_recv()
+            seqs = pl.ds(n * BATCH, BATCH)
+            a = half[seqs, pl.ds(pl.multiple_of(x * 8, 8), 8), :].reshape(BATCH * 8, 1152)
+            r = half_in[seqs].reshape(BATCH * 8, 1152)
+            parts, stats = merge_parts(a, r)
+            inv = 1.0 / stats[:, 8:16]
+            o = jnp.concatenate([parts[h] * inv[:, h:h + 1] for h in range(8)], axis=1).astype(jnp.bfloat16)
+            for y in range(2):
+                proj[n, y] = jnp.dot(o, wo_ref[:, y * 1024:(y + 1) * 1024], preferred_element_type=jnp.float32)
+            y_copy(n).start()
+
+        n_y, now_y = batch_of(LAG_Y)
+
+        @pl.when(now_y)
+        def _():
+            n = n_y
+            y_copy(n).wait_recv()
+            res = x_ref[pl.ds(n * BATCH, BATCH)].reshape(BATCH * 8, 1024).astype(jnp.float32)
+            gath[mine, n] = proj[n, tp] + proj_in[n] + res
+            gy_copy(n).start()
+            gx_copy(n).start()
+            c_copy(n, mine, 0).start()
+
+        n_g, now_g = batch_of(LAG_G)
+
+        @pl.when(now_g)
+        def _():
+            n = n_g
+            gy_copy(n).wait_recv()
+            dx_copy(n).start()
+            c_copy(n, from_y, 1).start()
+            gx_copy(n).wait_recv()
+            dy_copy(n).start()
+            c_copy(n, from_x, 2).start()
+
+        n_d, now_d = batch_of(LAG_D)
+
+        @pl.when(now_d)
+        def _():
+            n = n_d
+            dx_copy(n).wait_recv()
+            dy_copy(n).wait_recv()
+            c_copy(n, diag, 3).start()
+
+        n_f, now_f = batch_of(LAG_F)
+
+        @pl.when(now_f)
+        def _():
+            n = n_f
             for i in range(4):
-                head = 4 * pair + i
-                w_ref[b, :, head * 128:(head + 1) * 128] = out[i * 32:(i + 1) * 32, (i // 2) * 128:(i // 2 + 1) * 128]
-        w_ref[b, :, 1024:1152] = stat_tile(tops, 0) + stat_tile([o[1] for o in outs], 8)
-        return None if last else tuple(new_tops)
-
-    tops = lax.fori_loop(0, n_seq - 1, lambda b, t: step(b, t, False), tuple(tops))
-    step(n_seq - 1, tops, True)
-
-
-def attend(q, k_new, v_new, k_cache, v_cache, limits):
-    n_seq = q.shape[0]
+                c_copy(n, mine, i).wait_recv()
+            for kk in range(2):
+                for y in range(2):
+                    lo = gath[slot_of(0, y, kk), n].reshape(BATCH, 8, 1024)
+                    hi = gath[slot_of(1, y, kk), n].reshape(BATCH, 8, 1024)
+                    out_ref[pl.ds(n * BATCH, BATCH), kk * 16:(kk + 1) * 16, y * 1024:(y + 1) * 1024] = jnp.concatenate([lo, hi], axis=1).astype(jnp.bfloat16)
+
+        return carry
+
+    lax.fori_loop(0, N_SEQ + LAG_F - BATCH + 1, step, 0)
+
+    def drain_seq(b, carry):
+        core_copy(b).wait_send()
+        x_copy(b).wait_send()
+        return carry
+
+    def drain_batch(n, carry):
+        y_copy(n).wait_send()
+        gy_copy(n).wait_send()
+        gx_copy(n).wait_send()
+        dx_copy(n).wait_send()
+        dy_copy(n).wait_send()
+        for i in range(4):
+            c_copy(n, mine, i).wait_send()
+        return carry
+
+    lax.fori_loop(0, N_SEQ, drain_seq, 0)
+    lax.fori_loop(0, N_BATCH, drain_batch, 0)
+
+
+def block(q, k_new, v_new, resid, w_o, k_cache, v_cache, limits):
     rows = k_cache.shape[1] * 4
     vmem = pl.BlockSpec(memory_space=pltpu.VMEM)
+    hbm = pl.BlockSpec(memory_space=pl.ANY)
+    dma = pltpu.SemaphoreType.DMA
     return pl.pallas_call(
-        attend_kernel,
-        out_shape=jax.ShapeDtypeStruct((n_seq, 32, 1152), jnp.float32),
-        in_specs=[pl.BlockSpec(memory_space=pltpu.SMEM), vmem, vmem, vmem, pl.BlockSpec(memory_space=pl.ANY), pl.BlockSpec(memory_space=pl.ANY)],
+        block_kernel,
+        out_shape=jax.ShapeDtypeStruct((N_SEQ, 32, 2048), jnp.bfloat16),
+        in_specs=[pl.BlockSpec(memory_space=pltpu.SMEM), vmem, vmem, vmem, vmem, vmem, hbm, hbm],
         out_specs=vmem,
         scratch_shapes=[
             pltpu.VMEM((NBUF, rows, 128), jnp.bfloat16),
             pltpu.VMEM((NBUF, rows, 128), jnp.bfloat16),
             pltpu.VMEM((2, 2, 2048, 128), jnp.float32),
             pltpu.VMEM((2, 2, 32, 128), jnp.float32),
-            pltpu.SemaphoreType.DMA((NBUF,)),
-            pltpu.SemaphoreType.DMA((NBUF,)),
+            pltpu.VMEM((2, 2, 8, 128), jnp.float32),
+            pltpu.VMEM((N_SEQ, 32, 1152), jnp.float32),
+            pltpu.VMEM((N_SEQ, 16, 1152), jnp.float32),
+            pltpu.VMEM((N_SEQ, 16, 1152), jnp.float32),
+            pltpu.VMEM((N_SEQ, 8, 1152), jnp.float32),
+            pltpu.VMEM((N_BATCH, 2, BATCH * 8, 1024), jnp.float32),
+            pltpu.VMEM((N_BATCH, BATCH * 8, 1024), jnp.float32),
+            pltpu.VMEM((8, N_BATCH, BATCH * 8, 1024), jnp.float32),
+            dma((NBUF,)), dma((NBUF,)),
+            dma((N_SEQ,)), dma((N_SEQ,)), dma((N_SEQ,)), dma((N_SEQ,)),
+            dma((N_BATCH,)), dma((N_BATCH,)), dma((N_BATCH,)), dma((N_BATCH,)), dma((N_BATCH,)), dma((N_BATCH,)),
+            dma((N_BATCH,)), dma((N_BATCH,)), dma((N_BATCH,)), dma((N_BATCH,)), dma((4, N_BATCH)), dma((4, N_BATCH)),
         ],
-        compiler_params=pltpu.CompilerParams(vmem_limit_bytes=48 * 1024 * 1024),
-        cost_estimate=pl.CostEstimate(flops=17_000_000_000, bytes_accessed=140_000_000, transcendentals=17_000_000),
-    )(limits, q, k_new.reshape(n_seq, 128, 128), v_new.reshape(n_seq, 128, 128), k_cache.reshape(n_seq, rows, 128), v_cache.reshape(n_seq, rows, 128))
+        compiler_params=pltpu.CompilerParams(vmem_limit_bytes=62 * 1024 * 1024, collective_id=0, has_side_effects=True),
+        cost_estimate=pl.CostEstimate(flops=19_000_000_000, bytes_accessed=140_000_000, transcendentals=17_000_000),
+    )(limits, q, k_new.reshape(N_SEQ, 128, 128), v_new.reshape(N_SEQ, 128, 128), resid, w_o, k_cache.reshape(N_SEQ, rows, 128), v_cache.reshape(N_SEQ, rows, 128))
 
 
 def solution(mesh):
     def per_device(hidden, prefix_len, k_cache, v_cache, attn_norm, w_q, w_k, w_v, w_o, q_norm, k_norm):
-        n_seq, n_new, d_model = hidden.shape
         cp = lax.axis_index('cp')
         tp = lax.axis_index('tp')
         q_rot, k_new, v_new = project_new(hidden, attn_norm, w_q, w_k, w_v, q_norm, k_norm, prefix_len)
         limits = jnp.concatenate([prefix_len - cp * 2048, jnp.where(cp == 3, 0, 64)[None]]).astype(jnp.int32)
-        w = attend(q_rot.reshape(n_seq, n_new, 1024), k_new, v_new, k_cache, v_cache, limits)
-
-        def swap(array, axis, bit):
-            count = mesh.shape[axis]
-            return lax.ppermute(array, axis, [(i, i ^ bit) for i in range(count)])
-
-        def keep_send(array, which):
-            half = array.shape[1] // 2
-            first, second = array[:, :half], array[:, half:]
-            return jnp.where(which == 0, first, second), jnp.where(which == 0, second, first)
-
-        def merge(a, b):
-            ma, mb = a[..., 1024:1032], b[..., 1024:1032]
-            m = jnp.maximum(ma, mb)
-            scale = HEAD_DIM ** -0.5 * LOG2E
-            fa, fb = jnp.exp2((ma - m) * scale), jnp.exp2((mb - m) * scale)
-            shape = a.shape[:2] + (8, 128)
-            w = a[..., :1024].reshape(shape) * fa[..., None] + b[..., :1024].reshape(shape) * fb[..., None]
-            l = a[..., 1032:1040] * fa + b[..., 1032:1040] * fb
-            return w, m, l
-
-        def pack(w, m, l):
-            rest = jnp.zeros(m.shape[:2] + (112,), jnp.float32)
-            return jnp.concatenate([w.reshape(w.shape[:2] + (1024,)), m, l, rest], axis=-1)
-
-        keep, send = keep_send(w, cp % 2)
-        half = pack(*merge(keep, swap(send, 'cp', 1)))
-        keep, send = keep_send(half, cp // 2)
-        w4, _, l4 = merge(keep, swap(send, 'cp', 2))
-        o = (w4 / l4[..., None]).astype(jnp.bfloat16).reshape(n_seq * 8, 1024)
-        part = jnp.dot(o, w_o, preferred_element_type=jnp.float32)
-        first, second = part[:, :1024], part[:, 1024:]
-        mine = jnp.where(tp == 0, first, second) + swap(jnp.where(tp == 0, second, first), 'tp', 1)
-        ay = swap(mine, 'tp', 1)
-        ax = swap(mine, 'cp', 2)
-        dh = mine.shape[0] // 2
-        d0 = swap(ay[:dh], 'cp', 2)
-        d1 = swap(ax[dh:], 'tp', 1)
-        diag = jnp.concatenate([d0, d1], axis=0)
-        x_mine = jnp.concatenate([jnp.where(tp == 0, mine, ay), jnp.where(tp == 0, ay, mine)], axis=1)
-        x_other = jnp.concatenate([jnp.where(tp == 0, ax, diag), jnp.where(tp == 0, diag, ax)], axis=1)
-        x_mine = x_mine.reshape(n_seq, 8, d_model)
-        x_other = x_other.reshape(n_seq, 8, d_model)
-        x = cp // 2
-        core = jnp.concatenate([jnp.where(x == 0, x_mine, x_other), jnp.where(x == 0, x_other, x_mine)], axis=1)
-        peer = swap(core, 'cp', 1)
-        k = cp % 2
-        total = jnp.concatenate([jnp.where(k == 0, core, peer), jnp.where(k == 0, peer, core)], axis=1)
-        block_out = (hidden.astype(jnp.float32) + total).astype(jnp.bfloat16)
+        first = (cp % 2) * 16 + (cp // 2) * 8
+        resid = lax.dynamic_slice(hidden, (0, first, tp * 1024), (N_SEQ, 8, 1024))
+        block_out = block(q_rot.reshape(N_SEQ, 32, 1024), k_new, v_new, resid, w_o, k_cache, v_cache, limits)
         return block_out, k_new, v_new
 
     cache_spec = P('dp', 'cp', 'tp', None)

time: 255 us -> 163 us (0.64)
  waiting for transfers between devices: 84.8 us -> 0 us
  Pallas kernels: 60.9 us -> 101 us
  other arithmetic: 49.8 us -> 25.2 us
  starting transfers between devices: 11.2 us -> 0 us
  matrix products: 21.7 us -> 15.4 us
  local copies, waits for them, and re-layouts: 24.8 us -> 20 us
    ppermute x8 -> x0, waiting for transfers between devices: 84.8 us -> none  [swap(): return lax.ppermute(array, axis, [(i, i ^ bit) for i in range(count)])]
    pallas_call x1, Pallas kernels: 60.9 us -> 101 us  [block(): pl.pallas_call(block_kernel, out_shape=jax.ShapeDtypeStruct((N_SEQ, 32, 2...]
    ppermute x8 -> x0, starting transfers between devices: 11.2 us -> none  [swap(): return lax.ppermute(array, axis, [(i, i ^ bit) for i in range(count)])]
    select_n x7 -> x0, other arithmetic: 9.7 us -> none  [the longest x2 5.27 us: keep_send(): jnp.where(which == 0, first, second)]
    mul x4 -> x0, local copies, waits for them, and re-layouts: 9.33 us -> none  [the longest x2 4.69 us: merge(): a[..., :1024].reshape(shape) * fa[..., None]]
    add x4 -> x0, other arithmetic: 6.81 us -> none  [the longest x1 5.15 us: merge(): a[..., :1024].reshape(shape) * fa[..., None]]
    unnamed x18 -> x16, local copies, waits for them, and re-layouts: 1.09 us -> 7.78 us
    dot_general x1 -> x0, matrix products: 4.02 us -> none  [per_device(): part = jnp.dot(o, w_o, preferred_element_type=jnp.float32)]
  transfers between devices with their start and end apart: 8 -> 0, of which waited for: 7 -> 0; matrix products, arithmetic and copies ran while one was open for 2% -> 0% of each run, Pallas kernels for 0% -> 0%
where the time goes in v2:
time: 163 us; the launch traced here: 162 us
  Pallas kernels  101 us (62%)
  other arithmetic  25.2 us (15%)
  local copies, waits for them, and re-layouts  20 us (12%)
  matrix products  15.4 us (9%)
    pallas_call x1, Pallas kernels, block(): pl.pallas_call(block_kernel, out_shape=jax.ShapeDtypeStruct((N_SEQ, 32, 2...  101 us
    unnamed x16, local copies, waits for them, and re-layouts  7.78 us
    dot_general x1, matrix products, project_new(): jnp.einsum('bce,ef->bcf', normed, w_k, preferred_element_type=jnp.float32)  6.59 us
    dot_general x1, matrix products, project_new(): jnp.einsum('bce,ef->bcf', normed, w_q, preferred_element_type=jnp.float32)  6.38 us
    concatenate x3, other arithmetic, rope_apply(): jnp.concatenate([lead_half * cos_t - tail_half * sin_t, tail_half * cos_t...  6.36 us
    reduce_sum x3, other arithmetic, rms_scale(): mean_sq = jnp.mean(jnp.square(tensor), axis=-1, keepdims=True)  6.17 us
    mul x2, other arithmetic, rms_scale(): return tensor * lax.rsqrt(mean_sq + 1e-06) * norm_gain  4 us
    another operation x2, other arithmetic  3.77 us

profile of v2, /device:TPU:0, one launch (start us, length us, event | category | flops | bytes accessed | tf_op | source)
XLA Modules:
  0.0 162.3 jit_solution(2843145317246282134)
XLA Ops:
  0.6 0.0 copy-start.1
  0.7 0.8 broadcast_subtract_fusion
  1.5 0.6 pad_add_fusion.limit_ref
  2.1 0.7 convert_element_type.57
  2.8 0.7 convert_element_type.52
  3.5 3.1 %fusion = f32[32,32]{1,0:T(8,128)S(1)} fusion(bf16[32,32,2048]{2,1,0:T(8,128)(2,1)} %param.11), kind=kLoop, calls=%fused_computation.2 | loop fusion | flops 6290432 | bytes 4198400 | tf_op jit(solution)/shard_map/reduce_sum | solution.py:19
  6.5 0.0 copy-done.1
  6.5 6.4 %convert_convert_fusion = f32[32,32,1024]{2,1,0:T(8,128)S(1)} fusion(bf16[2048,1024]{1,0:T(8,128)(2,1)} %param.16, bf16[32,32,2048]{2,1,0:T(8,128)(2,1)S(1)} %copy-done.1, f32[2048]{0:T(1024)S(1)} %convert_element_type.52, f32[32,32]{1,0:T(8,128)S(1)} %add_rsqrt_fusion.2), kind=kOutput, calls=%fused_computation.22 | convolution fusion | flops 4305453056 | bytes 12595200 | tf_op jit(solution)/shard_map/bce,ef->bcf/dot_general | solution.py:39
  12.9 1.0 copy.17
  14.0 1.1 fusion.3
  15.1 0.1 add_rsqrt_fusion
  15.2 0.0 copy-start.4
  15.2 1.3 fusion.4
  16.5 0.0 copy-done.4
  16.5 0.1 add_convert_fusion.2
  16.6 1.9 %multiply_cosine_fusion = (f32[32,32,64]{2,1,0:T(8,128)S(1)}, f32[32,32,64]{2,1,0:T(8,128)S(1)}) fusion(f32[64]{0:T(128)S(1)} %negate_power_fusion, f32[32,32]{1,0:T(8,128)S(1)} %add_convert_fusion.2), kind=kLoop, calls=%fused_computation.29 | loop fusion | flops 65536 | bytes 528640 | tf_op jit(solution)/shard_map/cos | solution.py:27
  18.5 2.0 %subtract_convert_fusion = (bf16[32,32,8,64]{3,2,1,0:T(8,128)(2,1)S(1)}, bf16[32,32,8,64]{3,2,1,0:T(8,128)(2,1)S(1)}) fusion(f32[32,32,8,128]{3,2,1,0:T(8,128)S(1)} %fusion.4, f32[32,32,64]{2,1,0:T(8,128)S(1)} %get-tuple-element.8, f32[32,32,64]{2,1,0:T(8,128)S(1)} %get-tuple-element.7), kind=kLoop, calls=%fused_computation.12 | loop fusion | flops 4194304 | bytes 6815744 | tf_op jit(solution)/shard_map/convert.8
  20.4 1.2 pad_maximum_fusion
  21.6 2.3 %convert_element_type.59.q_ref = bf16[32,32,1024]{2,1,0:T(8,128)(2,1)} reshape(bf16[32,32,8,128]{3,2,1,0:T(8,128)(2,1)S(1)} %pad_maximum_fusion) | data formatting | bytes 4194304 | tf_op jit(solution)/shard_map/convert_element_type | solution.py:45
  23.9 6.6 %fusion.23 = f32[32,32,512]{2,1,0:T(8,128)} fusion(bf16[2048,512]{1,0:T(8,128)(2,1)} %param.17, bf16[32,32,2048]{2,1,0:T(8,128)(2,1)} %param.11, f32[2048]{0:T(1024)S(1)} %convert_element_type.52, f32[32,32]{1,0:T(8,128)S(1)} %add_rsqrt_fusion.2), kind=kOutput, calls=%fused_computation.24 | convolution fusion | flops 2156920832 | bytes 8400896 | tf_op jit(solution)/shard_map/bce,ef->bcf/dot_general | solution.py:40
  30.5 0.0 copy-start.6
  30.5 2.1 %reshape.91 = f32[32,32,4,128]{3,2,1,0:T(4,128)S(1)} reshape(f32[32,32,512]{2,1,0:T(8,128)} %fusion.23) | data formatting | bytes 4194304 | tf_op jit(solution)/shard_map/convert_element_type | solution.py:44
  32.6 0.0 copy-done.6
  32.6 2.0 %multiply_reduce_fusion = f32[32,32,4]{2,1,0:T(8,128)} fusion(f32[32,32,4,128]{3,2,1,0:T(4,128)S(1)} %reshape.91), kind=kLoop, calls=%fused_computation.21 | loop fusion | flops 1044480 | bytes 2113536 | tf_op jit(solution)/shard_map/reduce_sum | solution.py:19
  34.6 1.3 copy.15
  36.0 1.1 copy.16
  37.0 2.7 %multiply_multiply_fusion = f32[32,32,4,128]{3,2,1,0:T(4,128)S(1)} fusion(f32[32,32,4,128]{3,2,1,0:T(4,128)S(1)} %reshape.91, f32[128]{0:T(128)S(1)} %convert_element_type.63, f32[32,32,4]{2,1,0:T(8,128)} %copy.16), kind=kLoop, calls=%fused_computation.20 | loop fusion | flops 1048576 | bytes 4211200 | tf_op jit(solution)/shard_map/mul | solution.py:20
  39.8 0.0 copy-start.2
  39.8 0.0 copy-start.5
  39.8 1.8 %subtract_convert_fusion.1 = (bf16[32,32,4,64]{3,2,1,0:T(4,128)(2,1)S(1)}, bf16[32,32,4,64]{3,2,1,0:T(4,128)(2,1)S(1)}) fusion(f32[32,32,4,128]{3,2,1,0:T(4,128)S(1)} %multiply_multiply_fusion, f32[32,32,64]{2,1,0:T(8,128)S(1)} %get-tuple-element.8, f32[32,32,64]{2,1,0:T(8,128)S(1)} %get-tuple-element.7), kind=kLoop, calls=%fused_computation.19 | loop fusion | flops 2097152 | bytes 3670016 | tf_op jit(solution)/shard_map/convert.7
  41.6 0.0 copy-start
  41.6 1.0 copy-done
  42.6 1.6 pad_maximum_fusion.1.kn_ref
  44.2 0.0 copy-done.2
  44.2 0.0 copy-done.5
  44.2 2.4 %fusion.28 = bf16[32,32,512]{2,1,0:T(8,128)(2,1)S(1)} fusion(bf16[2048,512]{1,0:T(8,128)(2,1)S(1)} %copy-done.5, bf16[32,32,2048]{2,1,0:T(8,128)(2,1)S(1)} %copy-done.2, f32[2048]{0:T(1024)S(1)} %convert_element_type.52, f32[32,32]{1,0:T(8,128)S(1)} %add_rsqrt_fusion.2), kind=kOutput, calls=%fused_computation.25 | convolution fusion | flops 2156396544 | bytes 7352320 | tf_op jit(solution)/shard_map/bce,ef->bcf/dot_general | solution.py:41
  46.6 0.0 copy-start.3
  46.6 1.0 copy-done.3
  47.6 1.4 reshape_reshape.3.vn_ref
  49.0 1.9 %constant_dynamic-slice_fusion.x_ref = bf16[32,8,1024]{2,1,0:T(8,128)(2,1)} fusion(bf16[32,32,2048]{2,1,0:T(8,128)(2,1)} %param.11, s32[]{:T(128)S(6)} %select_n.24, s32[]{:T(128)S(6)} %select_n.25), kind=kLoop, calls=%fused_computation.36 | loop fusion | bytes 1048584 | tf_op jit(solution)/shard_map/dynamic_slice | solution.py:373
  50.9 100.9 %shard_map.130 = bf16[32,32,2048]{2,1,0:T(8,128)(2,1)} custom-call(s32[33]{0:T(128)} %pad_add_fusion.limit_ref, bf16[32,32,1024]{2,1,0:T(8,128)(2,1)} %convert_element_type.59.q_ref, bf16[32,128,128]{2,1,0:T(8,128)(2,1)} %pad_maximum_fusion.1.kn_ref, bf16[32,128,128]{2,1,0:T(8,128)(2,1)} %reshape_reshape.3.vn_ref, ...), custom_call_target="tpu_custom_call" | custom-call | flops 19000000512 | bytes 140000000 | tf_op jit(solution)/shard_map/pallas_call | solution.py:338
  151.7 3.6 %pad_maximum_fusion.2 = bf16[32,32,4,128]{3,2,1,0:T(4,128)(2,1)} fusion(bf16[32,32,4,64]{3,2,1,0:T(4,128)(2,1)} %copy-done, bf16[32,32,4,64]{3,2,1,0:T(4,128)(2,1)S(1)} %get-tuple-element.5), kind=kLoop, calls=%fused_computation.27 | loop fusion | flops 2097152 | bytes 2097152 | tf_op jit(solution)/shard_map/concatenate | solution.py:31
  155.4 2.1 %reshape.89 = bf16[32,32,4,128]{3,2,1,0:T(4,128)(2,1)} reshape(bf16[32,32,512]{2,1,0:T(8,128)(2,1)} %copy-done.3) | data formatting | bytes 2097152 | tf_op jit(solution)/shard_map/reshape | solution.py:47
  157.5 4.8 %copy.19 = bf16[32,32,2048]{2,1,0:T(8,128)(2,1)} copy(bf16[32,32,2048]{2,1,0:T(8,128)(2,1)} %shard_map.130) | data formatting | bytes 8388608
  (4 shorter events, 0.0 us)
Async XLA Ops:
  0.6 5.9 %copy-start.1 = (bf16[32,32,2048]{2,1,0:T(8,128)(2,1)S(1)}, bf16[32,32,2048]{2,1,0:T(8,128)(2,1)}, u32[]{:S(2)}) copy-start(bf16[32,32,2048]{2,1,0:T(8,128)(2,1)} %param.11) | copy-start | bytes 12582916
  15.2 1.3 copy-start.4
  30.5 2.1 %copy-start.6 = (bf16[128]{0:T(256)(128)(2,1)S(1)}, bf16[128]{0:T(256)(128)(2,1)}, u32[]{:S(2)}) copy-start(bf16[128]{0:T(256)(128)(2,1)} %param.21) | copy-start | bytes 772
  39.8 4.4 %copy-start.2 = (bf16[32,32,2048]{2,1,0:T(8,128)(2,1)S(1)}, bf16[32,32,2048]{2,1,0:T(8,128)(2,1)}, u32[]{:S(2)}) copy-start(bf16[32,32,2048]{2,1,0:T(8,128)(2,1)} %param.11) | copy-start | bytes 12582916
  39.8 4.4 %copy-start.5 = (bf16[2048,512]{1,0:T(8,128)(2,1)S(1)}, bf16[2048,512]{1,0:T(8,128)(2,1)}, u32[]{:S(2)}) copy-start(bf16[2048,512]{1,0:T(8,128)(2,1)} %param.18) | copy-start | bytes 6291460
  41.6 1.0 copy-start
  46.6 1.0 copy-start.3

commit v3 on v2

--- a/solution.py
+++ b/solution.py
@@ -1,7 +1,6 @@
-import functools
-
 import jax
 import jax.numpy as jnp
+import numpy as np
 from jax import lax
 from jax.experimental import pallas as pl
 from jax.experimental.pallas import tpu as pltpu
@@ -12,40 +11,89 @@
 FLOOR = -1e38
 LOG2E = 1.4426950408889634
 NBUF = 3
-CHUNK = 512
-
-
-def rms_scale(tensor, norm_gain):
-    mean_sq = jnp.mean(jnp.square(tensor), axis=-1, keepdims=True)
-    return tensor * lax.rsqrt(mean_sq + 1e-6) * norm_gain
-
-
-def rope_apply(tensor, positions):
-    half_dim = HEAD_DIM // 2
-    inv_freq = 1.0 / (1000000.0 ** (jnp.arange(half_dim, dtype=jnp.float32) * 2.0 / HEAD_DIM))
-    angles = positions.astype(jnp.float32)[..., None] * inv_freq
-    cos_t = jnp.cos(angles)[..., None, :]
-    sin_t = jnp.sin(angles)[..., None, :]
-    lead_half = tensor[..., :half_dim]
-    tail_half = tensor[..., half_dim:]
-    return jnp.concatenate([lead_half * cos_t - tail_half * sin_t, tail_half * cos_t + lead_half * sin_t], axis=-1)
-
-
-def project_new(hidden, attn_norm, w_q, w_k, w_v, q_norm, k_norm, prefix_len):
-    n_seq, n_new, d_model = hidden.shape
-    kv_count = w_k.shape[1] // HEAD_DIM
-    head_count = w_q.shape[1] // HEAD_DIM
-    normed = rms_scale(hidden.astype(jnp.float32), attn_norm.astype(jnp.float32)).astype(jnp.bfloat16)
-    q_lin = jnp.einsum('bce,ef->bcf', normed, w_q, preferred_element_type=jnp.float32).astype(jnp.bfloat16)
-    k_lin = jnp.einsum('bce,ef->bcf', normed, w_k, preferred_element_type=jnp.float32).astype(jnp.bfloat16)
-    v_lin = jnp.einsum('bce,ef->bcf', normed, w_v, preferred_element_type=jnp.float32).astype(jnp.bfloat16)
-    positions = prefix_len[:, None] + jnp.arange(n_new, dtype=jnp.int32)[None, :]
-    q_heads = q_lin.reshape(n_seq, n_new, head_count, HEAD_DIM).astype(jnp.float32)
-    k_heads = k_lin.reshape(n_seq, n_new, kv_count, HEAD_DIM).astype(jnp.float32)
-    q_rot = rope_apply(rms_scale(q_heads, q_norm.astype(jnp.float32)), positions).astype(jnp.bfloat16)
-    k_new = rope_apply(rms_scale(k_heads, k_norm.astype(jnp.float32)), positions).astype(jnp.bfloat16)
-    v_new = v_lin.reshape(n_seq, n_new, kv_count, HEAD_DIM)
-    return q_rot, k_new, v_new
+CHUNK = 256
+SCALE = HEAD_DIM ** -0.5 * LOG2E
+
+
+def rope_tables(prefix_len):
+    inv_freq = 1e6 ** -(np.arange(HEAD_DIM) % 64 / 64.0)
+    token_angles = np.arange(32)[:, None] * inv_freq
+    off = np.concatenate([np.cos(token_angles), np.sin(token_angles)], axis=1).astype(np.float32)
+    angles = prefix_len.astype(jnp.float32)[:, None] * inv_freq.astype(np.float32)
+    return jnp.concatenate([jnp.cos(angles), jnp.sin(angles)], axis=1), jnp.asarray(off)
+
+
+def project_kernel(x_ref, gain_ref, wq_ref, wk_ref, wv_ref, qn_ref, kn_ref, base_ref, off_ref, q_out, k_out, v_out, normed, kf, vf, cos_t, sin_t):
+    i = pl.program_id(0)
+
+    @pl.when(i == 0)
+    def _():
+        gain = gain_ref[...].astype(jnp.float32)
+
+        def norm(m, carry):
+            rows = pl.ds(pl.multiple_of(m * 128, 128), 128)
+            t = x_ref[rows, :].astype(jnp.float32)
+            normed[rows, :] = (t * lax.rsqrt(jnp.mean(t * t, axis=1, keepdims=True) + 1e-6) * gain).astype(jnp.bfloat16)
+            return carry
+
+        lax.fori_loop(0, 8, norm, 0)
+        cb, sb = off_ref[:, :128], off_ref[:, 128:]
+        lane = lax.broadcasted_iota(jnp.int32, (32, 128), 1)
+        for b in range(32):
+            ca, sa = base_ref[b:b + 1, :128], base_ref[b:b + 1, 128:]
+            sin = sa * cb + ca * sb
+            cos_t[b * 32:(b + 1) * 32, :] = ca * cb - sa * sb
+            sin_t[b * 32:(b + 1) * 32, :] = jnp.where(lane < 64, -sin, sin)
+
+    def head(lin, gain, rows):
+        t = lin.astype(jnp.bfloat16).astype(jnp.float32)
+        t = t * lax.rsqrt(jnp.mean(t * t, axis=1, keepdims=True) + 1e-6) * gain
+        return (t * cos_t[rows, :] + pltpu.roll(t, 64, 1) * sin_t[rows, :]).astype(jnp.bfloat16)
+
+    qg = qn_ref[...].astype(jnp.float32)
+    kg = kn_ref[...].astype(jnp.float32)
+    wkv = jnp.concatenate([wk_ref[...], wv_ref[...]], axis=1)
+    for m in range(4):
+        rows = slice(m * 256, (m + 1) * 256)
+        q = jnp.dot(normed[rows, :], wq_ref[...], preferred_element_type=jnp.float32)
+        kv = jnp.dot(normed[rows, :], wkv, preferred_element_type=jnp.float32)
+        for g in range(2):
+            q_out[rows, g * 128:(g + 1) * 128] = head(q[:, g * 128:(g + 1) * 128], qg, rows)
+        spread = pl.ds(m * 1024 + i, 256, stride=4)
+        kf[spread, :] = head(kv[:, :128], kg, rows).astype(jnp.float32)
+        vf[spread, :] = kv[:, 128:]
+
+    @pl.when(i == 3)
+    def _():
+        def finish(m, carry):
+            rows = pl.ds(pl.multiple_of(m * 512, 512), 512)
+            k_out[rows, :] = kf[rows, :].astype(jnp.bfloat16)
+            v_out[rows, :] = vf[rows, :].astype(jnp.bfloat16)
+            return carry
+
+        lax.fori_loop(0, 8, finish, 0)
+
+
+def project(hidden, attn_norm, w_q, w_k, w_v, q_norm, k_norm, prefix_len):
+    base, off = rope_tables(prefix_len)
+    whole = lambda shape: pl.BlockSpec(shape, lambda i: (0, 0))
+    cols = lambda n, w: pl.BlockSpec((n, w), lambda i: (0, i))
+    return pl.pallas_call(
+        project_kernel,
+        grid=(4,),
+        out_shape=(jax.ShapeDtypeStruct((1024, 1024), jnp.bfloat16), jax.ShapeDtypeStruct((4096, 128), jnp.bfloat16), jax.ShapeDtypeStruct((4096, 128), jnp.bfloat16)),
+        in_specs=[whole((1024, 2048)), whole((1, 2048)), cols(2048, 256), cols(2048, 128), cols(2048, 128), whole((1, 128)), whole((1, 128)), whole((32, 256)), whole((32, 256))],
+        out_specs=(cols(1024, 256), whole((4096, 128)), whole((4096, 128))),
+        scratch_shapes=[
+            pltpu.VMEM((1024, 2048), jnp.bfloat16),
+            pltpu.VMEM((4096, 128), jnp.float32),
+            pltpu.VMEM((4096, 128), jnp.float32),
+            pltpu.VMEM((1024, 128), jnp.float32),
+            pltpu.VMEM((1024, 128), jnp.float32),
+        ],
+        compiler_params=pltpu.CompilerParams(vmem_limit_bytes=40 * 1024 * 1024),
+        cost_estimate=pl.CostEstimate(flops=8_600_000_000, bytes_accessed=16_000_000, transcendentals=20_000),
+    )(hidden.reshape(1024, 2048), attn_norm.reshape(1, 2048), w_q, w_k, w_v, q_norm.reshape(1, 128), k_norm.reshape(1, 128), base, off)
 
 
 def head_rows(ref, start, count, head):
@@ -65,43 +113,44 @@
     return jnp.concatenate([top, low], axis=0).T
 
 
-def score_pass(q_ref, kn_ref, kbuf, scores, own_scores, b, limit, own):
-    tops = []
+def masked_scores(keys, wq, mask):
+    return jnp.where(mask, jnp.dot(keys, wq, preferred_element_type=jnp.float32), NEG)
+
+
+def fold_rows(op, tensor):
+    return op(tensor.reshape(tensor.shape[0] // 8, 8, 128), axis=0)
+
+
+def attend_step(q_ref, kn_ref, vn_ref, kbuf, vbuf, scores, own_scores, tops, b, nxt, limit, own):
     row = lax.broadcasted_iota(jnp.int32, (CHUNK, 128), 0)
-    own_row = lax.broadcasted_iota(jnp.int32, (32, 128), 0)
+    wq = [query_weights(q_ref, nxt, pair) for pair in range(2)]
+    new_top = [jnp.full((8, 128), FLOOR, jnp.float32) for _ in range(2)]
+    total = [jnp.zeros((8, 128), jnp.float32) for _ in range(2)]
+    out = [jnp.zeros((128, 256), jnp.float32) for _ in range(2)]
+
+    def values(pair, s, vals):
+        p = jnp.exp2((s - tops[pair]) * SCALE)
+        total[pair] = total[pair] + fold_rows(jnp.sum, p)
+        out[pair] = out[pair] + jnp.dot(p.astype(jnp.bfloat16).T, vals, preferred_element_type=jnp.float32)
+
+    for c in range(2048 // CHUNK):
+        rows = pl.ds(c * CHUNK, CHUNK)
+        mask = row < limit - c * CHUNK
+        for pair in range(2):
+            if tops is not None:
+                values(pair, scores[pair, rows, :], pair_rows(vbuf, c * CHUNK, CHUNK, pair))
+            s = masked_scores(pair_rows(kbuf, c * CHUNK, CHUNK, pair), wq[pair], mask)
+            scores[pair, rows, :] = s
+            new_top[pair] = jnp.maximum(new_top[pair], fold_rows(jnp.max, s))
     token = lax.broadcasted_iota(jnp.int32, (32, 128), 1) % 32
+    mask = lax.broadcasted_iota(jnp.int32, (32, 128), 0) <= token - own
     for pair in range(2):
-        wq = query_weights(q_ref, b, pair)
-        top = jnp.full((8, 128), FLOOR, jnp.float32)
-        for c in range(2048 // CHUNK):
-            s = jnp.dot(pair_rows(kbuf, c * CHUNK, CHUNK, pair), wq, preferred_element_type=jnp.float32)
-            s = jnp.where(row < limit - c * CHUNK, s, NEG)
-            scores[pair, pl.ds(c * CHUNK, CHUNK), :] = s
-            top = jnp.maximum(top, jnp.max(s.reshape(CHUNK // 8, 8, 128), axis=0))
-        s = jnp.dot(pair_rows(kn_ref.at[b], 0, 32, pair), wq, preferred_element_type=jnp.float32)
-        s = jnp.where(own_row <= token - own, s, NEG)
+        if tops is not None:
+            values(pair, own_scores[pair], pair_rows(vn_ref.at[b], 0, 32, pair))
+        s = masked_scores(pair_rows(kn_ref.at[nxt], 0, 32, pair), wq[pair], mask)
         own_scores[pair] = s
-        top = jnp.maximum(top, jnp.max(s.reshape(4, 8, 128), axis=0))
-        tops.append(jnp.max(top, axis=0, keepdims=True))
-    return tops
-
-
-def value_pass(vn_ref, vbuf, scores, own_scores, tops, b):
-    scale = HEAD_DIM ** -0.5 * LOG2E
-    outs = []
-    for pair in range(2):
-        top = tops[pair]
-        total = jnp.zeros((8, 128), jnp.float32)
-        out = jnp.zeros((128, 256), jnp.float32)
-        for c in range(2048 // CHUNK):
-            p = jnp.exp2((scores[pair, pl.ds(c * CHUNK, CHUNK), :] - top) * scale)
-            total = total + jnp.sum(p.reshape(CHUNK // 8, 8, 128), axis=0)
-            out = out + jnp.dot(p.astype(jnp.bfloat16).T, pair_rows(vbuf, c * CHUNK, CHUNK, pair), preferred_element_type=jnp.float32)
-        p = jnp.exp2((own_scores[pair] - top) * scale)
-        total = total + jnp.sum(p.reshape(4, 8, 128), axis=0)
-        out = out + jnp.dot(p.astype(jnp.bfloat16).T, pair_rows(vn_ref.at[b], 0, 32, pair), preferred_element_type=jnp.float32)
-        outs.append((out, jnp.sum(total, axis=0, keepdims=True)))
-    return outs
+        new_top[pair] = jnp.maximum(new_top[pair], fold_rows(jnp.max, s))
+    return out, [jnp.sum(t, axis=0, keepdims=True) for t in total], [jnp.max(t, axis=0, keepdims=True) for t in new_top]
 
 
 def stat_tile(rows, lane0):
@@ -118,7 +167,6 @@
 BATCH = 4
 N_BATCH = N_SEQ // BATCH
 LAG_X, LAG_Y, LAG_G, LAG_D, LAG_F = 6, 9, 13, 16, 18
-SCALE = HEAD_DIM ** -0.5 * LOG2E
 MESH = pl.DeviceIdType.MESH
 
 
@@ -136,9 +184,9 @@
     return parts, jnp.where(lane < 8, top, total)
 
 
-def block_kernel(limit_ref, q_ref, kn_ref, vn_ref, x_ref, wo_ref, k_hbm, v_hbm, out_ref,
-                 kbuf, vbuf, scores, own_scores, tops_ref, part, part_in, half, half_in, proj, proj_in, gath,
-                 ksem, vsem, d_send, d_recv, x_send, x_recv, y_send, y_recv, gx_send, gx_recv, gy_send, gy_recv,
+def block_kernel(prefix_ref, q_ref, kn_ref, vn_ref, wo_ref, x_hbm, k_hbm, v_hbm, out_ref,
+                 kbuf, vbuf, scores, own_scores, tops_ref, x_ref, part, part_in, half, half_in, proj, proj_in, gath,
+                 ksem, vsem, xsem, d_send, d_recv, x_send, x_recv, y_send, y_recv, gx_send, gx_recv, gy_send, gy_recv,
                  dx_send, dx_recv, dy_send, dy_recv, c_send, c_recv):
     dp, tp, cp = lax.axis_index('dp'), lax.axis_index('tp'), lax.axis_index('cp')
     x, k = cp // 2, cp % 2
@@ -193,21 +241,29 @@
     for b in range(NBUF - 1):
         for copy in copies(b):
             copy.start()
-    own = limit_ref[N_SEQ]
-
-    def run_scores(b, par):
-        tops = score_pass(q_ref, kn_ref, kbuf.at[lax.rem(b, NBUF)], scores.at[par], own_scores.at[par], b, limit_ref[b], own)
+    own = jnp.where(cp == 3, 0, 64)
+
+    first = k * 16 + x * 8
+    x_load = pltpu.make_async_copy(x_hbm.at[:, pl.ds(pl.multiple_of(first, 8), 8), pl.ds(pl.multiple_of(tp * 1024, 1024), 1024)], x_ref, xsem)
+    x_load.start()
+
+    def limit_of(b):
+        return prefix_ref[b] - cp * 2048
+
+    def keep_tops(tops):
         for pair in range(2):
-            tops_ref[par, pair] = jnp.broadcast_to(tops[pair], (8, 128))
+            tops_ref[pair] = jnp.broadcast_to(tops[pair], (8, 128))
 
     copies(0)[0].wait()
-    run_scores(0, 0)
+    keep_tops(attend_step(q_ref, kn_ref, vn_ref, kbuf.at[0], None, scores, own_scores, None, 0, 0, limit_of(0), own)[2])
     pl.semaphore_wait(barrier, 3)
+    x_load.wait()
 
     def step(it, carry):
         @pl.when(it < N_SEQ)
         def _():
-            b, par = it, lax.rem(it, 2)
+            b = it
+            nxt = jnp.minimum(b + 1, N_SEQ - 1)
             copies(b)[1].wait()
 
             @pl.when(b + 1 < N_SEQ)
@@ -219,15 +275,16 @@
                 for copy in copies(b + NBUF - 1):
                     copy.start()
 
-            run_scores(jnp.minimum(b + 1, N_SEQ - 1), 1 - par)
-            tops = [tops_ref[par, pair, 0:1, :] for pair in range(2)]
-            outs = value_pass(vn_ref, vbuf.at[lax.rem(b, NBUF)], scores.at[par], own_scores.at[par], tops, b)
+            tops = [tops_ref[pair, 0:1, :] for pair in range(2)]
+            outs, sums, new_tops = attend_step(q_ref, kn_ref, vn_ref, kbuf.at[lax.rem(nxt, NBUF)], vbuf.at[lax.rem(b, NBUF)], scores, own_scores,
+                                               tops, b, nxt, limit_of(nxt), own)
+            keep_tops(new_tops)
             for pair in range(2):
-                out = outs[pair][0]
+                out = outs[pair]
                 for i in range(4):
                     head = 4 * pair + i
                     part[b, :, head * 128:(head + 1) * 128] = out[i * 32:(i + 1) * 32, (i // 2) * 128:(i // 2 + 1) * 128]
-            part[b, :, 1024:1152] = stat_tile(tops, 0) + stat_tile([o[1] for o in outs], 8)
+            part[b, :, 1024:1152] = stat_tile(tops, 0) + stat_tile(sums, 8)
             core_copy(b).start()
 
         @pl.when((it >= 1) & (it < N_SEQ + 1))
@@ -330,7 +387,7 @@
     lax.fori_loop(0, N_BATCH, drain_batch, 0)
 
 
-def block(q, k_new, v_new, resid, w_o, k_cache, v_cache, limits):
+def block(q, k_rows, v_rows, hidden, w_o, k_cache, v_cache, prefix_len):
     rows = k_cache.shape[1] * 4
     vmem = pl.BlockSpec(memory_space=pltpu.VMEM)
     hbm = pl.BlockSpec(memory_space=pl.ANY)
@@ -338,14 +395,15 @@
     return pl.pallas_call(
         block_kernel,
         out_shape=jax.ShapeDtypeStruct((N_SEQ, 32, 2048), jnp.bfloat16),
-        in_specs=[pl.BlockSpec(memory_space=pltpu.SMEM), vmem, vmem, vmem, vmem, vmem, hbm, hbm],
+        in_specs=[pl.BlockSpec(memory_space=pltpu.SMEM), vmem, vmem, vmem, vmem, hbm, hbm, hbm],
         out_specs=vmem,
         scratch_shapes=[
             pltpu.VMEM((NBUF, rows, 128), jnp.bfloat16),
             pltpu.VMEM((NBUF, rows, 128), jnp.bfloat16),
-            pltpu.VMEM((2, 2, 2048, 128), jnp.float32),
-            pltpu.VMEM((2, 2, 32, 128), jnp.float32),
-            pltpu.VMEM((2, 2, 8, 128), jnp.float32),
+            pltpu.VMEM((2, 2048, 128), jnp.float32),
+            pltpu.VMEM((2, 32, 128), jnp.float32),
+            pltpu.VMEM((2, 8, 128), jnp.float32),
+            pltpu.VMEM((N_SEQ, 8, 1024), jnp.bfloat16),
             pltpu.VMEM((N_SEQ, 32, 1152), jnp.float32),
             pltpu.VMEM((N_SEQ, 16, 1152), jnp.float32),
             pltpu.VMEM((N_SEQ, 16, 1152), jnp.float32),
@@ -353,26 +411,21 @@
             pltpu.VMEM((N_BATCH, 2, BATCH * 8, 1024), jnp.float32),
             pltpu.VMEM((N_BATCH, BATCH * 8, 1024), jnp.float32),
             pltpu.VMEM((8, N_BATCH, BATCH * 8, 1024), jnp.float32),
-            dma((NBUF,)), dma((NBUF,)),
+            dma((NBUF,)), dma((NBUF,)), dma,
             dma((N_SEQ,)), dma((N_SEQ,)), dma((N_SEQ,)), dma((N_SEQ,)),
             dma((N_BATCH,)), dma((N_BATCH,)), dma((N_BATCH,)), dma((N_BATCH,)), dma((N_BATCH,)), dma((N_BATCH,)),
             dma((N_BATCH,)), dma((N_BATCH,)), dma((N_BATCH,)), dma((N_BATCH,)), dma((4, N_BATCH)), dma((4, N_BATCH)),
         ],
         compiler_params=pltpu.CompilerParams(vmem_limit_bytes=62 * 1024 * 1024, collective_id=0, has_side_effects=True),
         cost_estimate=pl.CostEstimate(flops=19_000_000_000, bytes_accessed=140_000_000, transcendentals=17_000_000),
-    )(limits, q, k_new.reshape(N_SEQ, 128, 128), v_new.reshape(N_SEQ, 128, 128), resid, w_o, k_cache.reshape(N_SEQ, rows, 128), v_cache.reshape(N_SEQ, rows, 128))
+    )(prefix_len, q, k_rows, v_rows, w_o, hidden, k_cache.reshape(N_SEQ, rows, 128), v_cache.reshape(N_SEQ, rows, 128))
 
 
 def solution(mesh):
     def per_device(hidden, prefix_len, k_cache, v_cache, attn_norm, w_q, w_k, w_v, w_o, q_norm, k_norm):
-        cp = lax.axis_index('cp')
-        tp = lax.axis_index('tp')
-        q_rot, k_new, v_new = project_new(hidden, attn_norm, w_q, w_k, w_v, q_norm, k_norm, prefix_len)
-        limits = jnp.concatenate([prefix_len - cp * 2048, jnp.where(cp == 3, 0, 64)[None]]).astype(jnp.int32)
-        first = (cp % 2) * 16 + (cp // 2) * 8
-        resid = lax.dynamic_slice(hidden, (0, first, tp * 1024), (N_SEQ, 8, 1024))
-        block_out = block(q_rot.reshape(N_SEQ, 32, 1024), k_new, v_new, resid, w_o, k_cache, v_cache, limits)
-        return block_out, k_new, v_new
+        q, k_rows, v_rows = project(hidden, attn_norm, w_q, w_k, w_v, q_norm, k_norm, prefix_len)
+        block_out = block(q.reshape(N_SEQ, 32, 1024), k_rows.reshape(N_SEQ, 128, 128), v_rows.reshape(N_SEQ, 128, 128), hidden, w_o, k_cache, v_cache, prefix_len)
+        return block_out, k_rows.reshape(N_SEQ, 32, 4, 128), v_rows.reshape(N_SEQ, 32, 4, 128)
 
     cache_spec = P('dp', 'cp', 'tp', None)
     arg_specs = (P('dp', None, None), P('dp'), cache_spec, cache_spec, P(None), P(None, 'tp'), P(None, 'tp'), P(None, 'tp'), P('tp', None), P(None), P(None))

time: 163 us -> 129 us (0.79)
  other arithmetic: 25.2 us -> 1.46 us
  matrix products: 15.4 us -> 0 us
  Pallas kernels: 101 us -> 112 us
  local copies, waits for them, and re-layouts: 20 us -> 14.2 us
    pallas_call x0 -> x1, Pallas kernels: none -> 15.6 us  [project(): pl.pallas_call(project_kernel, grid=(4,), out_shape=(jax.ShapeDtypeStruct...]
    dot_general x3 -> x0, matrix products: 15.4 us -> none  [the longest x1 6.59 us: project_new(): jnp.einsum('bce,ef->bcf', normed, w_k, preferred_element_type=jnp.float32)]
    concatenate x4 -> x1, other arithmetic: 7 us -> 0.01 us  [rope_tables(): jnp.concatenate([jnp.cos(angles), jnp.sin(angles)], axis=1)]
    reduce_sum x3 -> x0, other arithmetic: 6.17 us -> none  [rms_scale(): mean_sq = jnp.mean(jnp.square(tensor), axis=-1, keepdims=True)]
    unnamed x16 -> x15, local copies, waits for them, and re-layouts: 7.78 us -> 13.5 us
    pallas_call x1, Pallas kernels: 101 us -> 96.4 us  [block(): pl.pallas_call(block_kernel, out_shape=jax.ShapeDtypeStruct((N_SEQ, 32, 2...]
    convert_element_type x2 -> x0, local copies, waits for them, and re-layouts: 4.42 us -> none  [the longest x1 2.29 us: project_new(): rope_apply(rms_scale(q_heads, q_norm.astype(jnp.float32)), positions)]
    mul x2 -> x0, other arithmetic: 4 us -> none  [rms_scale(): return tensor * lax.rsqrt(mean_sq + 1e-06) * norm_gain]
where the time goes in v3:
time: 129 us; the launch traced here: 128 us
  Pallas kernels  112 us (87%)
  local copies, waits for them, and re-layouts  14.2 us (11%)
  other arithmetic  1.46 us (1%)
    pallas_call x1, Pallas kernels, block(): pl.pallas_call(block_kernel, out_shape=jax.ShapeDtypeStruct((N_SEQ, 32, 2...  96.4 us
    pallas_call x1, Pallas kernels, project(): pl.pallas_call(project_kernel, grid=(4,), out_shape=(jax.ShapeDtypeStruct...  15.6 us
    unnamed x15, local copies, waits for them, and re-layouts  13.5 us

profile of v3, /device:TPU:0, one launch (start us, length us, event | category | flops | bytes accessed | tf_op | source)
XLA Modules:
  0.0 128.3 jit_solution(17319925204361589068)
XLA Ops:
  0.6 0.7 convert_element_type.3
  1.3 0.7 reshape.42.gain_ref
  2.0 0.8 multiply_cosine_fusion
  2.8 0.0 copy-start
  2.8 2.2 %copy-done = bf16[32,32,2048]{2,1,0:T(8,128)(2,1)S(1)} copy-done((bf16[32,32,2048]{2,1,0:T(8,128)(2,1)S(1)}, bf16[32,32,2048]{2,1,0:T(8,128)(2,1)}, u32[]{:S(2)}) %copy-start) | copy-done | bytes 4194328
  5.0 0.0 copy-start.2
  5.0 1.6 %copy-done.2 = bf16[2048,512]{1,0:T(8,128)(2,1)S(1)} copy-done((bf16[2048,512]{1,0:T(8,128)(2,1)S(1)}, bf16[2048,512]{1,0:T(8,128)(2,1)}, u32[]{:S(2)}) %copy-start.2) | copy-done | bytes 2097176
  6.6 0.0 copy-start.3
  6.6 1.6 %copy-done.3 = bf16[2048,512]{1,0:T(8,128)(2,1)S(1)} copy-done((bf16[2048,512]{1,0:T(8,128)(2,1)S(1)}, bf16[2048,512]{1,0:T(8,128)(2,1)}, u32[]{:S(2)}) %copy-start.3) | copy-done | bytes 2097176
  8.2 0.0 copy-start.4
  8.2 0.7 copy-done.4
  8.8 0.0 copy-start.5
  8.8 0.7 copy-done.5
  9.5 0.0 copy-start.6
  9.5 0.8 copy-done.6
  10.2 15.6 %shard_map.148 = (bf16[1024,1024]{1,0:T(8,128)(2,1)S(1)}, bf16[4096,128]{1,0:T(8,128)(2,1)}, bf16[4096,128]{1,0:T(8,128)(2,1)}) custom-call(bf16[1024,2048]{1,0:T(8,128)(2,1)S(1)} %bitcast.10, bf16[1,2048]{1,0:T(2,128)(2,1)S(1)} %reshape.42.gain_ref, bf16[2048,1024]{1,0:T(8,128)(2,1)} %wq_ref.1, bf16[2048,512]{1,0:T(8,128)(2,1)S(1)} %copy-done.2, ...), custom_call_target="tpu_custom_call" | custom-call | flops 8600000512 | bytes 16000000 | tf_op jit(solution)/shard_map/pallas_call | solution.py:81
  25.8 0.0 copy-start.1
  25.8 1.3 %copy-done.1 = bf16[1024,1024]{1,0:T(8,128)(2,1)} copy-done((bf16[1024,1024]{1,0:T(8,128)(2,1)}, bf16[1024,1024]{1,0:T(8,128)(2,1)S(1)}, u32[]{:S(2)}) %copy-start.1) | copy-done | bytes 2097176
  27.1 96.4 %shard_map.149 = bf16[32,32,2048]{2,1,0:T(8,128)(2,1)} custom-call(s32[32]{0:T(128)} %prefix_ref.1, bf16[32,32,1024]{2,1,0:T(8,128)(2,1)} %bitcast.11, bf16[32,128,128]{2,1,0:T(8,128)(2,1)} %bitcast.14, bf16[32,128,128]{2,1,0:T(8,128)(2,1)} %bitcast.16, bf16[1024,2048]{1,0:T(8,128)(2,1)} %wo_ref.1, bf16[32,32,2048]{2,1,0:T(8,128)(2,1)} %x_hbm.1, ...), custom_call_target="tpu_custom_call" | custom-call | flops 19000000512 | bytes 140000000 | tf_op jit(solution)/shard_map/pallas_call | solution.py:395
  123.5 4.8 %copy.17 = bf16[32,32,2048]{2,1,0:T(8,128)(2,1)} copy(bf16[32,32,2048]{2,1,0:T(8,128)(2,1)} %shard_map.149) | data formatting | bytes 8388608
  (1 shorter events, 0.0 us)
Async XLA Ops:
  2.8 2.2 %copy-start = (bf16[32,32,2048]{2,1,0:T(8,128)(2,1)S(1)}, bf16[32,32,2048]{2,1,0:T(8,128)(2,1)}, u32[]{:S(2)}) copy-start(bf16[32,32,2048]{2,1,0:T(8,128)(2,1)} %x_hbm.1) | copy-start | bytes 12582916
  5.0 1.6 %copy-start.2 = (bf16[2048,512]{1,0:T(8,128)(2,1)S(1)}, bf16[2048,512]{1,0:T(8,128)(2,1)}, u32[]{:S(2)}) copy-start(bf16[2048,512]{1,0:T(8,128)(2,1)} %wk_ref.1) | copy-start | bytes 6291460
  6.6 1.6 %copy-start.3 = (bf16[2048,512]{1,0:T(8,128)(2,1)S(1)}, bf16[2048,512]{1,0:T(8,128)(2,1)}, u32[]{:S(2)}) copy-start(bf16[2048,512]{1,0:T(8,128)(2,1)} %wv_ref.1) | copy-start | bytes 6291460
  8.2 0.7 copy-start.4
  8.8 0.7 copy-start.5
  9.5 0.8 copy-start.6
  25.8 1.3 %copy-start.1 = (bf16[1024,1024]{1,0:T(8,128)(2,1)}, bf16[1024,1024]{1,0:T(8,128)(2,1)S(1)}, u32[]{:S(2)}) copy-start(bf16[1024,1024]{1,0:T(8,128)(2,1)S(1)} %get-tuple-element.6) | copy-start | bytes 6291460

commit v4 on v3

v4 whole, which is shorter than its diff:
```python
import jax
import jax.numpy as jnp
import numpy as np
from jax import lax
from jax.experimental import pallas as pl
from jax.experimental.pallas import tpu as pltpu
from jax.sharding import PartitionSpec as P

HEAD_DIM = 128
NEG = -3e38
FLOOR = -1e38
LOG2E = 1.4426950408889634
NBUF = 4
CHUNK = 256
SCALE = HEAD_DIM ** -0.5 * LOG2E


def rope_tables(prefix_len):
    freq = (1.0 / 1e6 ** (np.arange(HEAD_DIM) % 64 / 64.0)).astype(np.float32)
    token_angles = np.arange(32, dtype=np.float32)[:, None] * freq
    wide = token_angles.astype(np.float64)
    off = np.concatenate([np.cos(wide), np.sin(wide)], axis=1).astype(np.float32)
    angles = prefix_len.astype(jnp.float32)[:, None] * freq
    return jnp.concatenate([jnp.cos(angles), jnp.sin(angles)], axis=1), jnp.asarray(off), jnp.asarray(freq[None])


def project_kernel(x_ref, gain_ref, wq_ref, wk_ref, wv_ref, qn_ref, kn_ref, base_ref, off_ref, freq_ref, prefix_ref, q_out, k_out, v_out, normed, kf, vf, cos_t, sin_t):
    i = pl.program_id(0)

    @pl.when(i == 0)
    def _():
        gain = gain_ref[...].astype(jnp.float32)

        def norm(m, carry):
            rows = pl.ds(pl.multiple_of(m * 128, 128), 128)
            t = x_ref[rows, :].astype(jnp.float32)
            normed[rows, :] = (t * lax.rsqrt(jnp.mean(t * t, axis=1, keepdims=True) + 1e-6) * gain).astype(jnp.bfloat16)
            return carry

        lax.fori_loop(0, 8, norm, 0)
        cb, sb = off_ref[:, :128], off_ref[:, 128:]
        freq = freq_ref[...]
        lane = lax.broadcasted_iota(jnp.int32, (32, 128), 1)
        token = lax.broadcasted_iota(jnp.int32, (32, 128), 0)
        token_angle = token.astype(jnp.float32) * freq
        for b in range(32):
            ca, sa = base_ref[b:b + 1, :128], base_ref[b:b + 1, 128:]
            prefix = prefix_ref[b]
            angle = (token + prefix).astype(jnp.float32) * freq
            base_angle = jnp.full((1, 128), prefix, jnp.int32).astype(jnp.float32) * freq
            eps = (angle - base_angle) - token_angle
            near = 1.0 - 0.5 * eps * eps
            ct, st = cb * near - sb * eps, sb * near + cb * eps
            sin = sa * ct + ca * st
            cos_t[b * 32:(b + 1) * 32, :] = ca * ct - sa * st
            sin_t[b * 32:(b + 1) * 32, :] = jnp.where(lane < 64, -sin, sin)

    def head(lin, gain, rows):
        t = lin.astype(jnp.bfloat16).astype(jnp.float32)
        t = t * lax.rsqrt(jnp.mean(t * t, axis=1, keepdims=True) + 1e-6) * gain
        return (t * cos_t[rows, :] + pltpu.roll(t, 64, 1) * sin_t[rows, :]).astype(jnp.bfloat16)

    qg = qn_ref[...].astype(jnp.float32)
    kg = kn_ref[...].astype(jnp.float32)
    wkv = jnp.concatenate([wk_ref[...], wv_ref[...]], axis=1)
    for m in range(4):
        rows = slice(m * 256, (m + 1) * 256)
        q = jnp.dot(normed[rows, :], wq_ref[...], preferred_element_type=jnp.float32)
        kv = jnp.dot(normed[rows, :], wkv, preferred_element_type=jnp.float32)
        for g in range(2):
            q_out[rows, g * 128:(g + 1) * 128] = head(q[:, g * 128:(g + 1) * 128], qg, rows)
        spread = pl.ds(m * 1024 + i, 256, stride=4)
        kf[spread, :] = head(kv[:, :128], kg, rows).astype(jnp.float32)
        vf[spread, :] = kv[:, 128:]

    @pl.when(i == 3)
    def _():
        def finish(m, carry):
            rows = pl.ds(pl.multiple_of(m * 512, 512), 512)
            k_out[rows, :] = kf[rows, :].astype(jnp.bfloat16)
            v_out[rows, :] = vf[rows, :].astype(jnp.bfloat16)
            return carry

        lax.fori_loop(0, 8, finish, 0)


def project(hidden, attn_norm, w_q, w_k, w_v, q_norm, k_norm, prefix_len):
    base, off, freq = rope_tables(prefix_len)
    whole = lambda shape: pl.BlockSpec(shape, lambda i: (0, 0))
    cols = lambda n, w: pl.BlockSpec((n, w), lambda i: (0, i))
    return pl.pallas_call(
        project_kernel,
        grid=(4,),
        out_shape=(jax.ShapeDtypeStruct((1024, 1024), jnp.bfloat16), jax.ShapeDtypeStruct((4096, 128), jnp.bfloat16), jax.ShapeDtypeStruct((4096, 128), jnp.bfloat16)),
        in_specs=[whole((1024, 2048)), whole((1, 2048)), cols(2048, 256), cols(2048, 128), cols(2048, 128), whole((1, 128)), whole((1, 128)), whole((32, 256)), whole((32, 256)), whole((1, 128)), pl.BlockSpec(memory_space=pltpu.SMEM)],
        out_specs=(cols(1024, 256), whole((4096, 128)), whole((4096, 128))),
        scratch_shapes=[
            pltpu.VMEM((1024, 2048), jnp.bfloat16),
            pltpu.VMEM((4096, 128), jnp.float32),
            pltpu.VMEM((4096, 128), jnp.float32),
            pltpu.VMEM((1024, 128), jnp.float32),
            pltpu.VMEM((1024, 128), jnp.float32),
        ],
        compiler_params=pltpu.CompilerParams(vmem_limit_bytes=62 * 1024 * 1024),
        cost_estimate=pl.CostEstimate(flops=8_600_000_000, bytes_accessed=16_000_000, transcendentals=20_000),
    )(hidden.reshape(1024, 2048), attn_norm.reshape(1, 2048), w_q, w_k, w_v, q_norm.reshape(1, 128), k_norm.reshape(1, 128), base, off, freq, prefix_len)


def head_rows(ref, start, count, head):
    return ref[pl.ds(start * 4 + head, count, stride=4), :]


def pair_rows(ref, start, count, pair):
    return jnp.concatenate([head_rows(ref, start, count, 2 * pair), head_rows(ref, start, count, 2 * pair + 1)], axis=1)


def query_weights(q_ref, b, pair):
    def head(h):
        return jnp.concatenate([q_ref[b, :, (2 * h + g) * 128:(2 * h + g + 1) * 128] for g in range(2)], axis=0)
    zero = jnp.zeros((64, 128), jnp.bfloat16)
    top = jnp.concatenate([head(2 * pair), zero], axis=1)
    low = jnp.concatenate([zero, head(2 * pair + 1)], axis=1)
    return jnp.concatenate([top, low], axis=0).T


def masked_scores(keys, wq, mask):
    return jnp.where(mask, jnp.dot(keys, wq, preferred_element_type=jnp.float32), NEG)


def fold_rows(op, tensor):
    return op(tensor.reshape(tensor.shape[0] // 8, 8, 128), axis=0)


def attend_step(q_ref, kn_ref, vn_ref, kbuf, vbuf, scores, own_scores, tops, b, nxt, limit, own, between=()):
    row = lax.broadcasted_iota(jnp.int32, (CHUNK, 128), 0)
    wq = [query_weights(q_ref, nxt, pair) for pair in range(2)]
    new_top = [jnp.full((8, 128), FLOOR, jnp.float32) for _ in range(2)]
    total = [jnp.zeros((8, 128), jnp.float32) for _ in range(2)]
    out = [jnp.zeros((128, 256), jnp.float32) for _ in range(2)]

    def values(pair, s, vals):
        p = jnp.exp2((s - tops[pair]) * SCALE)
        total[pair] = total[pair] + fold_rows(jnp.sum, p)
        out[pair] = out[pair] + jnp.dot(p.astype(jnp.bfloat16).T, vals, preferred_element_type=jnp.float32)

    for c in range(2048 // CHUNK):
        rows = pl.ds(c * CHUNK, CHUNK)
        mask = row < limit - c * CHUNK
        for pair in range(2):
            if tops is not None:
                values(pair, scores[pair, rows, :], pair_rows(vbuf, c * CHUNK, CHUNK, pair))
            s = masked_scores(pair_rows(kbuf, c * CHUNK, CHUNK, pair), wq[pair], mask)
            scores[pair, rows, :] = s
            new_top[pair] = jnp.maximum(new_top[pair], fold_rows(jnp.max, s))
        for work in between[c::2048 // CHUNK]:
            work()
    token = lax.broadcasted_iota(jnp.int32, (32, 128), 1) % 32
    mask = lax.broadcasted_iota(jnp.int32, (32, 128), 0) <= token - own
    for pair in range(2):
        if tops is not None:
            values(pair, own_scores[pair], pair_rows(vn_ref.at[b], 0, 32, pair))
        s = masked_scores(pair_rows(kn_ref.at[nxt], 0, 32, pair), wq[pair], mask)
        own_scores[pair] = s
        new_top[pair] = jnp.maximum(new_top[pair], fold_rows(jnp.max, s))
    return out, [jnp.sum(t, axis=0, keepdims=True) for t in total], [jnp.max(t, axis=0, keepdims=True) for t in new_top]


def stat_tile(rows, lane0):
    lane = lax.broadcasted_iota(jnp.int32, (32, 128), 1)
    tile = jnp.zeros((32, 128), jnp.float32)
    for pair in range(2):
        col = jnp.broadcast_to(rows[pair], (128, 128)).T
        for i in range(4):
            tile = jnp.where(lane == lane0 + 4 * pair + i, col[i * 32:(i + 1) * 32], tile)
    return tile


N_SEQ = 32
BATCH = 2
N_BATCH = N_SEQ // BATCH
LAG_X, LAG_Y, LAG_G, LAG_D, LAG_F = 6, 9, 14, 18, 21
MESH = pl.DeviceIdType.MESH


def merge_parts(a, r):
    sa, sr = a[:, 1024:], r[:, 1024:]
    lane = lax.broadcasted_iota(jnp.int32, sa.shape, 1)
    top = jnp.maximum(sa, sr)
    fa = jnp.where(lane < 8, jnp.exp2((sa - top) * SCALE), 0.0)
    fr = jnp.where(lane < 8, jnp.exp2((sr - top) * SCALE), 0.0)
    total = sa * pltpu.roll(fa, 8, 1) + sr * pltpu.roll(fr, 8, 1)
    parts = []
    for h in range(8):
        cols = slice(h * 128, (h + 1) * 128)
        parts.append(a[:, cols] * fa[:, h:h + 1] + r[:, cols] * fr[:, h:h + 1])
    return parts, jnp.where(lane < 8, top, total)


def block_kernel(prefix_ref, q_ref, kn_ref, vn_ref, wo_hbm, x_hbm, k_hbm, v_hbm, out_ref,
                 kbuf, vbuf, scores, own_scores, tops_ref, x_ref, wo_ref, part, part_in, half, half_in, proj, proj_in, gath,
                 ksem, vsem, xsem, wsem, d_send, d_recv, x_send, x_recv, y_send, y_recv, gx_send, gx_recv, gy_send, gy_recv,
                 g_send, g_recv, c_send, c_recv):
    dp, tp, cp = lax.axis_index('dp'), lax.axis_index('tp'), lax.axis_index('cp')
    x, k = cp // 2, cp % 2
    core_peer = (dp, tp, cp + 1 - 2 * k)
    x_peer = (dp, tp, cp + 2 - 4 * x)
    y_peer = (dp, 1 - tp, cp)

    barrier = pltpu.get_barrier_semaphore()
    for peer in (core_peer, x_peer, y_peer):
        pl.semaphore_signal(barrier, inc=1, device_id=peer, device_id_type=MESH)

    def copies(b):
        slot = lax.rem(b, NBUF)
        return (pltpu.make_async_copy(k_hbm.at[b], kbuf.at[slot], ksem.at[slot]),
                pltpu.make_async_copy(v_hbm.at[b], vbuf.at[slot], vsem.at[slot]))

    def remote(src, dst, send, recv, peer):
        return pltpu.make_async_remote_copy(src_ref=src, dst_ref=dst, send_sem=send, recv_sem=recv, device_id=peer, device_id_type=MESH)

    def core_copy(b):
        return remote(part.at[b, pl.ds(pl.multiple_of((1 - k) * 16, 16), 16)], part_in.at[b], d_send.at[b], d_recv.at[b], core_peer)

    def x_copy(b):
        return remote(half.at[b, pl.ds(pl.multiple_of((1 - x) * 8, 8), 8)], half_in.at[b], x_send.at[b], x_recv.at[b], x_peer)

    def y_copy(n):
        return remote(proj.at[n, 1 - tp], proj_in.at[n], y_send.at[n], y_recv.at[n], y_peer)

    mine, from_x, from_y = x * 2 + tp, (1 - x) * 2 + tp, x * 2 + 1 - tp

    def gath_copy(s, slot, send, recv, peer):
        return remote(gath.at[s, k, slot], gath.at[s, k, slot], send.at[s], recv.at[s], peer)

    def gx_copy(s):
        return gath_copy(s, mine, gx_send, gx_recv, x_peer)

    def gy_copy(s):
        return gath_copy(s, mine, gy_send, gy_recv, y_peer)

    def diag_copy(s, odd):
        if odd:
            return gath_copy(s, from_x, g_send, g_recv, y_peer)
        return gath_copy(s, from_y, g_send, g_recv, x_peer)

    def c_copy(s):
        return remote(gath.at[s, k], gath.at[s, k], c_send.at[s], c_recv.at[s], core_peer)

    for b in range(NBUF - 1):
        for copy in copies(b):
            copy.start()
    own = jnp.where(cp == 3, 0, 64)

    first = k * 16 + x * 8
    x_load = pltpu.make_async_copy(x_hbm.at[:, pl.ds(pl.multiple_of(first, 8), 8), pl.ds(pl.multiple_of(tp * 1024, 1024), 1024)], x_ref, xsem)
    x_load.start()
    wo_load = pltpu.make_async_copy(wo_hbm, wo_ref, wsem)
    wo_load.start()

    def limit_of(b):
        return prefix_ref[b] - cp * 2048

    def keep_tops(tops):
        for pair in range(2):
            tops_ref[pair] = jnp.broadcast_to(tops[pair], (8, 128))

    copies(0)[0].wait()
    keep_tops(attend_step(q_ref, kn_ref, vn_ref, kbuf.at[0], None, scores, own_scores, None, 0, 0, limit_of(0), own)[2])
    pl.semaphore_wait(barrier, 3)
    x_load.wait()
    wo_load.wait()

    def merge_core(b):
        parts, stats = merge_parts(part[jnp.minimum(b, N_SEQ - 1), pl.ds(pl.multiple_of(k * 16, 16), 16), :], part_in[b])
        for h in range(8):
            half[b, :, h * 128:(h + 1) * 128] = parts[h]
        half[b, :, 1024:] = stats

    def wait_x(n):
        for i in range(BATCH):
            x_copy(n * BATCH + i).wait_recv()

    def normalized(n):
        seqs = pl.ds(n * BATCH, BATCH)
        a = half[seqs, pl.ds(pl.multiple_of(x * 8, 8), 8), :].reshape(BATCH * 8, 1152)
        r = half_in[seqs].reshape(BATCH * 8, 1152)
        parts, stats = merge_parts(a, r)
        inv = 1.0 / stats[:, 8:16]
        return jnp.concatenate([parts[h] * inv[:, h:h + 1] for h in range(8)], axis=1).astype(jnp.bfloat16)

    def project_part(n, o, y, q):
        lo = y * 1024 + q * 512
        proj[n, y, :, q * 512:(q + 1) * 512] = jnp.dot(o, wo_ref[:, lo:lo + 512], preferred_element_type=jnp.float32)

    def project_out(n):
        o = normalized(n)
        for y in range(2):
            for q in range(2):
                project_part(n, o, y, q)

    def add_peer(n):
        res = x_ref[pl.ds(jnp.minimum(n, N_BATCH - 1) * BATCH, BATCH)].reshape(BATCH * 8, 1024).astype(jnp.float32)
        gath[pl.ds(n * BATCH, BATCH), k, mine] = (proj[n, tp] + proj_in[n] + res).reshape(BATCH, 8, 1024)

    def send_mine(s):
        gy_copy(s).start()
        gx_copy(s).start()

    def forward(s, odd):
        gy_copy(s).wait_recv()
        gx_copy(s).wait_recv()
        diag_copy(s, odd).start()

    def forward_core(s, odd):
        diag_copy(s, odd).wait_recv()
        c_copy(s).start()

    def finish(s):
        at = jnp.minimum(s, N_SEQ - 1)
        for kk in range(2):
            for y in range(2):
                both = jnp.concatenate([gath[s, kk, y], gath[s, kk, 2 + y]], axis=0)
                out_ref[at, kk * 16:(kk + 1) * 16, y * 1024:(y + 1) * 1024] = both.astype(jnp.bfloat16)

    at_x, at_y = (divmod(lag, BATCH)[::-1] for lag in (LAG_X, LAG_Y))

    def batch_step(n, carry):
        def behind(at):
            return jnp.where(n >= at[1], n - at[1], N_BATCH)

        for j in range(BATCH):
            b = n * BATCH + j
            nxt = jnp.minimum(b + 1, N_SEQ - 1)

            def lagged(lag, b=b):
                return jnp.where(b >= lag, b - lag, N_SEQ)

            copies(b)[1].wait()

            @pl.when(b + 1 < N_SEQ)
            def _():
                copies(b + 1)[0].wait()

            @pl.when(b + NBUF - 1 < N_SEQ)
            def _():
                for copy in copies(b + NBUF - 1):
                    copy.start()

            @pl.when(b >= 2)
            def _():
                core_copy(b - 2).wait_recv()

            if at_x[0] == j:
                @pl.when(n >= at_x[1])
                def _():
                    wait_x(n - at_x[1])
            if at_y[0] == j:
                @pl.when(n >= at_y[1])
                def _():
                    y_copy(n - at_y[1]).wait_recv()

            @pl.when(b >= LAG_G)
            def _():
                forward(b - LAG_G, (j - LAG_G) % 2)

            @pl.when(b >= LAG_D)
            def _():
                forward_core(b - LAG_D, (j - LAG_D) % 2)

            @pl.when(b >= LAG_F)
            def _():
                c_copy(b - LAG_F).wait_recv()

            between = [lambda b=b: merge_core(lagged(2, b)), lambda b=b: finish(lagged(LAG_F, b))]
            if at_y[0] == j:
                between.append(lambda: add_peer(behind(at_y)))
            if at_x[0] == j:
                parts_of = normalized(behind(at_x))
                between += [lambda y=y, q=q: project_part(behind(at_x), parts_of, y, q) for y in range(2) for q in range(2)]
            tops = [tops_ref[pair, 0:1, :] for pair in range(2)]
            outs, sums, new_tops = attend_step(q_ref, kn_ref, vn_ref, kbuf.at[lax.rem(nxt, NBUF)], vbuf.at[lax.rem(b, NBUF)], scores, own_scores,
                                               tops, b, nxt, limit_of(nxt), own, between)
            keep_tops(new_tops)
            for pair in range(2):
                out = outs[pair]
                for i in range(4):
                    head = 4 * pair + i
                    part[b, :, head * 128:(head + 1) * 128] = out[i * 32:(i + 1) * 32, (i // 2) * 128:(i // 2 + 1) * 128]
            part[b, :, 1024:1152] = stat_tile(tops, 0) + stat_tile(sums, 8)
            core_copy(b).start()

            @pl.when(b >= 2)
            def _():
                x_copy(b - 2).start()

            if at_x[0] == j:
                @pl.when(n >= at_x[1])
                def _():
                    y_copy(n - at_x[1]).start()

            @pl.when(b >= LAG_Y)
            def _():
                send_mine(b - LAG_Y)
        return carry

    lax.fori_loop(0, N_BATCH, batch_step, 0)

    for b in range(N_SEQ, N_SEQ + LAG_F):
        if b - 2 < N_SEQ:
            core_copy(b - 2).wait_recv()
            merge_core(b - 2)
            x_copy(b - 2).start()
        if b - LAG_G < N_SEQ:
            forward(b - LAG_G, (b - LAG_G) % 2)
        if b - LAG_D < N_SEQ:
            forward_core(b - LAG_D, (b - LAG_D) % 2)
        if (b - LAG_X) % BATCH == 0 and (b - LAG_X) < N_SEQ:
            n = (b - LAG_X) // BATCH
            wait_x(n)
            project_out(n)
            y_copy(n).start()
        if (b - LAG_Y) % BATCH == 0 and (b - LAG_Y) < N_SEQ:
            n = (b - LAG_Y) // BATCH
            y_copy(n).wait_recv()
            add_peer(n)
        if b - LAG_Y < N_SEQ:
            send_mine(b - LAG_Y)
        c_copy(b - LAG_F).wait_recv()
        finish(b - LAG_F)

    def drain(b, carry):
        for copy in (core_copy(b), x_copy(b), gx_copy(b), gy_copy(b), diag_copy(b, 0), c_copy(b)):
            copy.wait_send()
        return carry

    def drain_y(n, carry):
        y_copy(n).wait_send()
        return carry

    lax.fori_loop(0, N_SEQ, drain, 0)
    lax.fori_loop(0, N_BATCH, drain_y, 0)


def block(q, k_rows, v_rows, hidden, w_o, k_cache, v_cache, prefix_len):
    rows = k_cache.shape[1] * 4
    vmem = pl.BlockSpec(memory_space=pltpu.VMEM)
    hbm = pl.BlockSpec(memory_space=pl.ANY)
    dma = pltpu.SemaphoreType.DMA
    return pl.pallas_call(
        block_kernel,
        out_shape=jax.ShapeDtypeStruct((N_SEQ, 32, 2048), jnp.bfloat16),
        in_specs=[pl.BlockSpec(memory_space=pltpu.SMEM), vmem, vmem, vmem, hbm, hbm, hbm, hbm],
        out_specs=vmem,
        scratch_shapes=[
            pltpu.VMEM((NBUF, rows, 128), jnp.bfloat16),
            pltpu.VMEM((NBUF, rows, 128), jnp.bfloat16),
            pltpu.VMEM((2, 2048, 128), jnp.float32),
            pltpu.VMEM((2, 32, 128), jnp.float32),
            pltpu.VMEM((2, 8, 128), jnp.float32),
            pltpu.VMEM((N_SEQ, 8, 1024), jnp.bfloat16),
            pltpu.VMEM((1024, 2048), jnp.bfloat16),
            pltpu.VMEM((N_SEQ, 32, 1152), jnp.float32),
            pltpu.VMEM((N_SEQ + 1, 16, 1152), jnp.float32),
            pltpu.VMEM((N_SEQ + BATCH, 16, 1152), jnp.float32),
            pltpu.VMEM((N_SEQ + BATCH, 8, 1152), jnp.float32),
            pltpu.VMEM((N_BATCH + 1, 2, BATCH * 8, 1024), jnp.float32),
            pltpu.VMEM((N_BATCH + 1, BATCH * 8, 1024), jnp.float32),
            pltpu.VMEM((N_SEQ + BATCH, 2, 4, 8, 1024), jnp.float32),
            dma((NBUF,)), dma((NBUF,)), dma, dma,
            dma((N_SEQ,)), dma((N_SEQ,)), dma((N_SEQ,)), dma((N_SEQ,)),
            dma((N_BATCH,)), dma((N_BATCH,)), *[dma((N_SEQ,))] * 8,
        ],
        compiler_params=pltpu.CompilerParams(vmem_limit_bytes=60 * 1024 * 1024, collective_id=0, has_side_effects=True),
        cost_estimate=pl.CostEstimate(flops=19_000_000_000, bytes_accessed=140_000_000, transcendentals=17_000_000),
    )(prefix_len, q, k_rows, v_rows, w_o, hidden, k_cache.reshape(N_SEQ, rows, 128), v_cache.reshape(N_SEQ, rows, 128))


def solution(mesh):
    def per_device(hidden, prefix_len, k_cache, v_cache, attn_norm, w_q, w_k, w_v, w_o, q_norm, k_norm):
        q, k_rows, v_rows = project(hidden, attn_norm, w_q, w_k, w_v, q_norm, k_norm, prefix_len)
        block_out = block(q.reshape(N_SEQ, 32, 1024), k_rows.reshape(N_SEQ, 128, 128), v_rows.reshape(N_SEQ, 128, 128), hidden, w_o, k_cache, v_cache, prefix_len)
        return block_out, k_rows.reshape(N_SEQ, 32, 4, 128), v_rows.reshape(N_SEQ, 32, 4, 128)

    cache_spec = P('dp', 'cp', 'tp', None)
    arg_specs = (P('dp', None, None), P('dp'), cache_spec, cache_spec, P(None), P(None, 'tp'), P(None, 'tp'), P(None, 'tp'), P('tp', None), P(None), P(None))
    out_specs = (P('dp', None, None), P('dp', None, 'tp', None), P('dp', None, 'tp', None))
    return jax.shard_map(per_device, mesh=mesh, in_specs=arg_specs, out_specs=out_specs, check_vma=False)
```

time: 129 us -> 118 us (0.915)
  local copies, waits for them, and re-layouts: 14.2 us -> 6.07 us
  Pallas kernels: 112 us -> 109 us
    unnamed x15 -> x1, local copies, waits for them, and re-layouts: 13.5 us -> 4.79 us
    pallas_call x1, Pallas kernels: 96.4 us -> 91.9 us  [block(): pl.pallas_call(block_kernel, out_shape=jax.ShapeDtypeStruct((N_SEQ, 32, 2...]
    pallas_call x1, Pallas kernels: 15.6 us -> 17.4 us  [project(): pl.pallas_call(project_kernel, grid=(4,), out_shape=(jax.ShapeDtypeStruct...]
where the time goes in v4:
time: 118 us
  Pallas kernels  109 us (92%)
  local copies, waits for them, and re-layouts  6.07 us (5%)
  other arithmetic  2.06 us (2%)
    pallas_call x1, Pallas kernels, block(): pl.pallas_call(block_kernel, out_shape=jax.ShapeDtypeStruct((N_SEQ, 32, 2...  91.9 us
    pallas_call x1, Pallas kernels, project(): pl.pallas_call(project_kernel, grid=(4,), out_shape=(jax.ShapeDtypeStruct...  17.4 us
    unnamed x1, local copies, waits for them, and re-layouts  4.79 us

profile of v4, /device:TPU:0, one launch (start us, length us, event | category | flops | bytes accessed | tf_op | source)
XLA Modules:
  0.0 118.1 jit_solution(1983458387752471107)
XLA Ops:
  0.6 0.7 convert_element_type.3
  1.3 1.3 %reshape.42.gain_ref = bf16[1,2048]{1,0:T(2,128)(2,1)} reshape(bf16[2048]{0:T(1024)(128)(2,1)} %param.18) | data formatting | bytes 8192 | tf_op jit(solution)/shard_map/reshape | solution.py:106
  2.6 0.8 multiply_cosine_fusion
  3.4 0.6 pad_maximum_fusion.base_ref
  4.0 17.4 %shard_map.157 = (bf16[1024,1024]{1,0:T(8,128)(2,1)}, bf16[4096,128]{1,0:T(8,128)(2,1)}, bf16[4096,128]{1,0:T(8,128)(2,1)}) custom-call(bf16[1024,2048]{1,0:T(8,128)(2,1)} %bitcast.10, bf16[1,2048]{1,0:T(2,128)(2,1)} %reshape.42.gain_ref, bf16[2048,1024]{1,0:T(8,128)(2,1)} %wq_ref.1, bf16[2048,512]{1,0:T(8,128)(2,1)} %wk_ref.1, bf16[2048,512]{1,0:T(8,128)(2,1)} %wv_ref.1, ...), custom_call_target="tpu_custom_call" | custom-call | flops 8600000512 | bytes 16000000 | tf_op jit(solution)/shard_map/pallas_call | solution.py:91
  21.4 91.9 %shard_map.158 = bf16[32,32,2048]{2,1,0:T(8,128)(2,1)} custom-call(s32[32]{0:T(128)} %prefix_ref.3, bf16[32,32,1024]{2,1,0:T(8,128)(2,1)} %bitcast.11, bf16[32,128,128]{2,1,0:T(8,128)(2,1)} %bitcast.12, bf16[32,128,128]{2,1,0:T(8,128)(2,1)} %bitcast.14, bf16[1024,2048]{1,0:T(8,128)(2,1)} %wo_hbm.1, bf16[32,32,2048]{2,1,0:T(8,128)(2,1)} %x_hbm.1, ...), custom_call_target="tpu_custom_call" | custom-call | flops 19000000512 | bytes 140000000 | tf_op jit(solution)/shard_map/pallas_call | solution.py:449
  113.3 4.8 %copy.18 = bf16[32,32,2048]{2,1,0:T(8,128)(2,1)} copy(bf16[32,32,2048]{2,1,0:T(8,128)(2,1)} %shard_map.158) | data formatting | bytes 8388608

commit v5 on v4

--- a/solution.py
+++ b/solution.py
@@ -24,26 +24,24 @@
     return jnp.concatenate([jnp.cos(angles), jnp.sin(angles)], axis=1), jnp.asarray(off), jnp.asarray(freq[None])
 
 
-def project_kernel(x_ref, gain_ref, wq_ref, wk_ref, wv_ref, qn_ref, kn_ref, base_ref, off_ref, freq_ref, prefix_ref, q_out, k_out, v_out, normed, kf, vf, cos_t, sin_t):
-    i = pl.program_id(0)
-
-    @pl.when(i == 0)
-    def _():
+def project_kernel(x_hbm, gain_ref, wq_ref, wk_ref, wv_ref, qn_ref, kn_ref, base_ref, off_ref, freq_ref, prefix_ref, q_out, k_out, v_out,
+                   x_ref, normed, kf, vf, cos_t, sin_t, xsem):
+    def load(m):
+        return pltpu.make_async_copy(x_hbm.at[pl.ds(m * 256, 256)], x_ref.at[m], xsem.at[m])
+
+    def prepare(m):
+        load(m).wait()
         gain = gain_ref[...].astype(jnp.float32)
-
-        def norm(m, carry):
-            rows = pl.ds(pl.multiple_of(m * 128, 128), 128)
-            t = x_ref[rows, :].astype(jnp.float32)
-            normed[rows, :] = (t * lax.rsqrt(jnp.mean(t * t, axis=1, keepdims=True) + 1e-6) * gain).astype(jnp.bfloat16)
-            return carry
-
-        lax.fori_loop(0, 8, norm, 0)
+        for part in range(2):
+            t = x_ref[m, part * 128:(part + 1) * 128, :].astype(jnp.float32)
+            t = t * lax.rsqrt(jnp.mean(t * t, axis=1, keepdims=True) + 1e-6) * gain
+            normed[m * 256 + part * 128:m * 256 + (part + 1) * 128, :] = t.astype(jnp.bfloat16)
         cb, sb = off_ref[:, :128], off_ref[:, 128:]
         freq = freq_ref[...]
         lane = lax.broadcasted_iota(jnp.int32, (32, 128), 1)
         token = lax.broadcasted_iota(jnp.int32, (32, 128), 0)
         token_angle = token.astype(jnp.float32) * freq
-        for b in range(32):
+        for b in range(m * 8, m * 8 + 8):
             ca, sa = base_ref[b:b + 1, :128], base_ref[b:b + 1, 128:]
             prefix = prefix_ref[b]
             angle = (token + prefix).astype(jnp.float32) * freq
@@ -60,28 +58,38 @@
         t = t * lax.rsqrt(jnp.mean(t * t, axis=1, keepdims=True) + 1e-6) * gain
         return (t * cos_t[rows, :] + pltpu.roll(t, 64, 1) * sin_t[rows, :]).astype(jnp.bfloat16)
 
-    qg = qn_ref[...].astype(jnp.float32)
-    kg = kn_ref[...].astype(jnp.float32)
-    wkv = jnp.concatenate([wk_ref[...], wv_ref[...]], axis=1)
-    for m in range(4):
-        rows = slice(m * 256, (m + 1) * 256)
-        q = jnp.dot(normed[rows, :], wq_ref[...], preferred_element_type=jnp.float32)
-        kv = jnp.dot(normed[rows, :], wkv, preferred_element_type=jnp.float32)
-        for g in range(2):
-            q_out[rows, g * 128:(g + 1) * 128] = head(q[:, g * 128:(g + 1) * 128], qg, rows)
-        spread = pl.ds(m * 1024 + i, 256, stride=4)
-        kf[spread, :] = head(kv[:, :128], kg, rows).astype(jnp.float32)
-        vf[spread, :] = kv[:, 128:]
-
-    @pl.when(i == 3)
-    def _():
-        def finish(m, carry):
-            rows = pl.ds(pl.multiple_of(m * 512, 512), 512)
-            k_out[rows, :] = kf[rows, :].astype(jnp.bfloat16)
-            v_out[rows, :] = vf[rows, :].astype(jnp.bfloat16)
-            return carry
-
-        lax.fori_loop(0, 8, finish, 0)
+    def run(i, first, last):
+        qg = qn_ref[...].astype(jnp.float32)
+        kg = kn_ref[...].astype(jnp.float32)
+        wkv = jnp.concatenate([wk_ref[...], wv_ref[...]], axis=1)
+        if first:
+            for m in range(4):
+                load(m).start()
+
+        def lines(m):
+            if first:
+                prepare(m)
+            lhs = normed[m * 256:(m + 1) * 256, :]
+            return jnp.dot(lhs, wq_ref[...], preferred_element_type=jnp.float32), jnp.dot(lhs, wkv, preferred_element_type=jnp.float32)
+
+        ahead = lines(0)
+        for m in range(4):
+            (q, kv), ahead = ahead, lines(m + 1) if m < 3 else None
+            rows = slice(m * 256, (m + 1) * 256)
+            for g in range(2):
+                q_out[rows, g * 128:(g + 1) * 128] = head(q[:, g * 128:(g + 1) * 128], qg, rows)
+            spread = pl.ds(m * 1024 + i, 256, stride=4)
+            kf[spread, :] = head(kv[:, :128], kg, rows).astype(jnp.float32)
+            vf[spread, :] = kv[:, 128:]
+            if last:
+                done = slice(m * 1024, (m + 1) * 1024)
+                k_out[done, :] = kf[done, :].astype(jnp.bfloat16)
+                v_out[done, :] = vf[done, :].astype(jnp.bfloat16)
+
+    i = pl.program_id(0)
+    pl.when(i == 0)(lambda: run(0, True, False))
+    pl.when((i > 0) & (i < 3))(lambda: run(i, False, False))
+    pl.when(i == 3)(lambda: run(3, False, True))
 
 
 def project(hidden, attn_norm, w_q, w_k, w_v, q_norm, k_norm, prefix_len):
@@ -92,14 +100,16 @@
         project_kernel,
         grid=(4,),
         out_shape=(jax.ShapeDtypeStruct((1024, 1024), jnp.bfloat16), jax.ShapeDtypeStruct((4096, 128), jnp.bfloat16), jax.ShapeDtypeStruct((4096, 128), jnp.bfloat16)),
-        in_specs=[whole((1024, 2048)), whole((1, 2048)), cols(2048, 256), cols(2048, 128), cols(2048, 128), whole((1, 128)), whole((1, 128)), whole((32, 256)), whole((32, 256)), whole((1, 128)), pl.BlockSpec(memory_space=pltpu.SMEM)],
+        in_specs=[pl.BlockSpec(memory_space=pl.ANY), whole((1, 2048)), cols(2048, 256), cols(2048, 128), cols(2048, 128), whole((1, 128)), whole((1, 128)), whole((32, 256)), whole((32, 256)), whole((1, 128)), pl.BlockSpec(memory_space=pltpu.SMEM)],
         out_specs=(cols(1024, 256), whole((4096, 128)), whole((4096, 128))),
         scratch_shapes=[
+            pltpu.VMEM((4, 256, 2048), jnp.bfloat16),
             pltpu.VMEM((1024, 2048), jnp.bfloat16),
             pltpu.VMEM((4096, 128), jnp.float32),
             pltpu.VMEM((4096, 128), jnp.float32),
             pltpu.VMEM((1024, 128), jnp.float32),
             pltpu.VMEM((1024, 128), jnp.float32),
+            pltpu.SemaphoreType.DMA((4,)),
         ],
         compiler_params=pltpu.CompilerParams(vmem_limit_bytes=62 * 1024 * 1024),
         cost_estimate=pl.CostEstimate(flops=8_600_000_000, bytes_accessed=16_000_000, transcendentals=20_000),
@@ -448,7 +458,7 @@
     dma = pltpu.SemaphoreType.DMA
     return pl.pallas_call(
         block_kernel,
-        out_shape=jax.ShapeDtypeStruct((N_SEQ, 32, 2048), jnp.bfloat16),
+        out_shape=pltpu.VMEM((N_SEQ, 32, 2048), jnp.bfloat16),
         in_specs=[pl.BlockSpec(memory_space=pltpu.SMEM), vmem, vmem, vmem, hbm, hbm, hbm, hbm],
         out_specs=vmem,
         scratch_shapes=[
@@ -470,7 +480,7 @@
             dma((N_SEQ,)), dma((N_SEQ,)), dma((N_SEQ,)), dma((N_SEQ,)),
             dma((N_BATCH,)), dma((N_BATCH,)), *[dma((N_SEQ,))] * 8,
         ],
-        compiler_params=pltpu.CompilerParams(vmem_limit_bytes=60 * 1024 * 1024, collective_id=0, has_side_effects=True),
+        compiler_params=pltpu.CompilerParams(vmem_limit_bytes=56 * 1024 * 1024, collective_id=0, has_side_effects=True),
         cost_estimate=pl.CostEstimate(flops=19_000_000_000, bytes_accessed=140_000_000, transcendentals=17_000_000),
     )(prefix_len, q, k_rows, v_rows, w_o, hidden, k_cache.reshape(N_SEQ, rows, 128), v_cache.reshape(N_SEQ, rows, 128))
 

time: 118 us -> 113 us (0.958)
  local copies, waits for them, and re-layouts: 6.07 us -> 3.3 us
  Pallas kernels: 109 us -> 107 us
    unnamed x1, local copies, waits for them, and re-layouts: 4.79 us -> 2.02 us
    pallas_call x1, Pallas kernels: 91.9 us -> 90 us  [block(): pl.pallas_call(block_kernel, out_shape=pltpu.VMEM((N_SEQ, 32, 2048), jnp....]
where the time goes in v5:
time: 113 us
  Pallas kernels  107 us (95%)
  local copies, waits for them, and re-layouts  3.3 us (3%)
  other arithmetic  2.06 us (2%)
    pallas_call x1, Pallas kernels, block(): pl.pallas_call(block_kernel, out_shape=pltpu.VMEM((N_SEQ, 32, 2048), jnp....  90 us
    pallas_call x1, Pallas kernels, project(): pl.pallas_call(project_kernel, grid=(4,), out_shape=(jax.ShapeDtypeStruct...  17.2 us

profile of v5, /device:TPU:0, one launch (start us, length us, event | category | flops | bytes accessed | tf_op | source)
XLA Modules:
  0.0 113.2 jit_solution(15322078492084220636)
XLA Ops:
  0.6 0.7 convert_element_type.3
  1.3 1.3 %reshape.42.gain_ref = bf16[1,2048]{1,0:T(2,128)(2,1)} reshape(bf16[2048]{0:T(1024)(128)(2,1)} %param.18) | data formatting | bytes 8192 | tf_op jit(solution)/shard_map/reshape | solution.py:116
  2.6 0.8 multiply_cosine_fusion
  3.4 0.6 pad_maximum_fusion.base_ref
  4.0 17.2 %shard_map.157 = (bf16[1024,1024]{1,0:T(8,128)(2,1)}, bf16[4096,128]{1,0:T(8,128)(2,1)}, bf16[4096,128]{1,0:T(8,128)(2,1)}) custom-call(bf16[1024,2048]{1,0:T(8,128)(2,1)} %bitcast.10, bf16[1,2048]{1,0:T(2,128)(2,1)} %reshape.42.gain_ref, bf16[2048,1024]{1,0:T(8,128)(2,1)} %wq_ref.1, bf16[2048,512]{1,0:T(8,128)(2,1)} %wk_ref.1, bf16[2048,512]{1,0:T(8,128)(2,1)} %wv_ref.1, ...), custom_call_target="tpu_custom_call" | custom-call | flops 8600000512 | bytes 16000000 | tf_op jit(solution)/shard_map/pallas_call | solution.py:99
  21.2 90.0 %shard_map.158 = bf16[32,32,2048]{2,1,0:T(8,128)(2,1)S(1)} custom-call(s32[32]{0:T(128)} %prefix_ref.3, bf16[32,32,1024]{2,1,0:T(8,128)(2,1)} %bitcast.11, bf16[32,128,128]{2,1,0:T(8,128)(2,1)} %bitcast.12, bf16[32,128,128]{2,1,0:T(8,128)(2,1)} %bitcast.14, bf16[1024,2048]{1,0:T(8,128)(2,1)} %wo_hbm.1, bf16[32,32,2048]{2,1,0:T(8,128)(2,1)} %x_hbm.1, ...), custom_call_target="tpu_custom_call" | custom-call | flops 19000000512 | bytes 140000000 | tf_op jit(solution)/shard_map/pallas_call | solution.py:459
  111.1 2.0 %copy.18 = bf16[32,32,2048]{2,1,0:T(8,128)(2,1)} copy(bf16[32,32,2048]{2,1,0:T(8,128)(2,1)S(1)} %shard_map.158) | data formatting | bytes 8388608

commit v6 on v5

--- a/solution.py
+++ b/solution.py
@@ -31,7 +31,7 @@
 
     def prepare(m):
         load(m).wait()
-        gain = gain_ref[...].astype(jnp.float32)
+        gain = gain_ref[...].astype(jnp.float32).reshape(1, 2048)
         for part in range(2):
             t = x_ref[m, part * 128:(part + 1) * 128, :].astype(jnp.float32)
             t = t * lax.rsqrt(jnp.mean(t * t, axis=1, keepdims=True) + 1e-6) * gain
@@ -100,7 +100,7 @@
         project_kernel,
         grid=(4,),
         out_shape=(jax.ShapeDtypeStruct((1024, 1024), jnp.bfloat16), jax.ShapeDtypeStruct((4096, 128), jnp.bfloat16), jax.ShapeDtypeStruct((4096, 128), jnp.bfloat16)),
-        in_specs=[pl.BlockSpec(memory_space=pl.ANY), whole((1, 2048)), cols(2048, 256), cols(2048, 128), cols(2048, 128), whole((1, 128)), whole((1, 128)), whole((32, 256)), whole((32, 256)), whole((1, 128)), pl.BlockSpec(memory_space=pltpu.SMEM)],
+        in_specs=[pl.BlockSpec(memory_space=pl.ANY), pl.BlockSpec((2048,), lambda i: (0,)), cols(2048, 256), cols(2048, 128), cols(2048, 128), whole((1, 128)), whole((1, 128)), whole((32, 256)), whole((32, 256)), whole((1, 128)), pl.BlockSpec(memory_space=pltpu.SMEM)],
         out_specs=(cols(1024, 256), whole((4096, 128)), whole((4096, 128))),
         scratch_shapes=[
             pltpu.VMEM((4, 256, 2048), jnp.bfloat16),
@@ -113,7 +113,7 @@
         ],
         compiler_params=pltpu.CompilerParams(vmem_limit_bytes=62 * 1024 * 1024),
         cost_estimate=pl.CostEstimate(flops=8_600_000_000, bytes_accessed=16_000_000, transcendentals=20_000),
-    )(hidden.reshape(1024, 2048), attn_norm.reshape(1, 2048), w_q, w_k, w_v, q_norm.reshape(1, 128), k_norm.reshape(1, 128), base, off, freq, prefix_len)
+    )(hidden.reshape(1024, 2048), attn_norm, w_q, w_k, w_v, q_norm.reshape(1, 128), k_norm.reshape(1, 128), base, off, freq, prefix_len)
 
 
 def head_rows(ref, start, count, head):
@@ -206,9 +206,9 @@
     return parts, jnp.where(lane < 8, top, total)
 
 
-def block_kernel(prefix_ref, q_ref, kn_ref, vn_ref, wo_hbm, x_hbm, k_hbm, v_hbm, out_ref,
-                 kbuf, vbuf, scores, own_scores, tops_ref, x_ref, wo_ref, part, part_in, half, half_in, proj, proj_in, gath,
-                 ksem, vsem, xsem, wsem, d_send, d_recv, x_send, x_recv, y_send, y_recv, gx_send, gx_recv, gy_send, gy_recv,
+def block_kernel(prefix_ref, q_hbm, kn_hbm, vn_hbm, wo_hbm, x_hbm, k_hbm, v_hbm, out_ref,
+                 kbuf, vbuf, scores, own_scores, tops_ref, x_ref, wo_ref, q_ref, kn_ref, vn_ref, part, part_in, half, half_in, proj, proj_in, gath,
+                 ksem, vsem, xsem, wsem, nsem, d_send, d_recv, x_send, x_recv, y_send, y_recv, gx_send, gx_recv, gy_send, gy_recv,
                  g_send, g_recv, c_send, c_recv):
     dp, tp, cp = lax.axis_index('dp'), lax.axis_index('tp'), lax.axis_index('cp')
     x, k = cp // 2, cp % 2
@@ -256,7 +256,12 @@
     def c_copy(s):
         return remote(gath.at[s, k], gath.at[s, k], c_send.at[s], c_recv.at[s], core_peer)
 
-    for b in range(NBUF - 1):
+    new_loads = [pltpu.make_async_copy(src, dst, nsem.at[i]) for i, (src, dst) in enumerate(((q_hbm, q_ref), (kn_hbm, kn_ref), (vn_hbm, vn_ref)))]
+    copies(0)[0].start()
+    for load in new_loads:
+        load.start()
+    copies(0)[1].start()
+    for b in range(1, NBUF - 1):
         for copy in copies(b):
             copy.start()
     own = jnp.where(cp == 3, 0, 64)
@@ -275,6 +280,8 @@
             tops_ref[pair] = jnp.broadcast_to(tops[pair], (8, 128))
 
     copies(0)[0].wait()
+    for load in new_loads:
+        load.wait()
     keep_tops(attend_step(q_ref, kn_ref, vn_ref, kbuf.at[0], None, scores, own_scores, None, 0, 0, limit_of(0), own)[2])
     pl.semaphore_wait(barrier, 3)
     x_load.wait()
@@ -459,7 +466,7 @@
     return pl.pallas_call(
         block_kernel,
         out_shape=pltpu.VMEM((N_SEQ, 32, 2048), jnp.bfloat16),
-        in_specs=[pl.BlockSpec(memory_space=pltpu.SMEM), vmem, vmem, vmem, hbm, hbm, hbm, hbm],
+        in_specs=[pl.BlockSpec(memory_space=pltpu.SMEM), *[hbm] * 7],
         out_specs=vmem,
         scratch_shapes=[
             pltpu.VMEM((NBUF, rows, 128), jnp.bfloat16),
@@ -469,6 +476,9 @@
             pltpu.VMEM((2, 8, 128), jnp.float32),
             pltpu.VMEM((N_SEQ, 8, 1024), jnp.bfloat16),
             pltpu.VMEM((1024, 2048), jnp.bfloat16),
+            pltpu.VMEM((N_SEQ, 32, 1024), jnp.bfloat16),
+            pltpu.VMEM((N_SEQ, 128, 128), jnp.bfloat16),
+            pltpu.VMEM((N_SEQ, 128, 128), jnp.bfloat16),
             pltpu.VMEM((N_SEQ, 32, 1152), jnp.float32),
             pltpu.VMEM((N_SEQ + 1, 16, 1152), jnp.float32),
             pltpu.VMEM((N_SEQ + BATCH, 16, 1152), jnp.float32),
@@ -476,7 +486,7 @@
             pltpu.VMEM((N_BATCH + 1, 2, BATCH * 8, 1024), jnp.float32),
             pltpu.VMEM((N_BATCH + 1, BATCH * 8, 1024), jnp.float32),
             pltpu.VMEM((N_SEQ + BATCH, 2, 4, 8, 1024), jnp.float32),
-            dma((NBUF,)), dma((NBUF,)), dma, dma,
+            dma((NBUF,)), dma((NBUF,)), dma, dma, dma((3,)),
             dma((N_SEQ,)), dma((N_SEQ,)), dma((N_SEQ,)), dma((N_SEQ,)),
             dma((N_BATCH,)), dma((N_BATCH,)), *[dma((N_SEQ,))] * 8,
         ],

time: 113 us -> 112 us (level)
  local copies, waits for them, and re-layouts: 3.3 us -> 2.02 us
    reshape x1 -> x0, local copies, waits for them, and re-layouts: 1.28 us -> none  [project(): attn_norm.reshape(1, 2048)]
where the time goes in v6:
time: 112 us
  Pallas kernels  107 us (96%)
  other arithmetic  2.06 us (2%)
  local copies, waits for them, and re-layouts  2.02 us (2%)
    pallas_call x1, Pallas kernels, block(): pl.pallas_call(block_kernel, out_shape=pltpu.VMEM((N_SEQ, 32, 2048), jnp....  89.7 us
    pallas_call x1, Pallas kernels, project(): pl.pallas_call(project_kernel, grid=(4,), out_shape=(jax.ShapeDtypeStruct...  17.2 us

profile of v6, /device:TPU:0, one launch (start us, length us, event | category | flops | bytes accessed | tf_op | source)
XLA Modules:
  0.0 111.6 jit_solution(13578922925573097250)
XLA Ops:
  0.6 0.7 convert_element_type.3
  1.3 0.8 multiply_cosine_fusion
  2.1 0.6 pad_maximum_fusion.base_ref
  2.7 17.2 %shard_map.157 = (bf16[1024,1024]{1,0:T(8,128)(2,1)}, bf16[4096,128]{1,0:T(8,128)(2,1)}, bf16[4096,128]{1,0:T(8,128)(2,1)}) custom-call(bf16[1024,2048]{1,0:T(8,128)(2,1)} %bitcast.10, bf16[2048]{0:T(1024)(128)(2,1)} %gain_ref.1, bf16[2048,1024]{1,0:T(8,128)(2,1)} %wq_ref.1, bf16[2048,512]{1,0:T(8,128)(2,1)} %wk_ref.1, bf16[2048,512]{1,0:T(8,128)(2,1)} %wv_ref.1, ...), custom_call_target="tpu_custom_call" | custom-call | flops 8600000512 | bytes 16000000 | tf_op jit(solution)/shard_map/pallas_call | solution.py:99
  19.9 89.7 %shard_map.158 = bf16[32,32,2048]{2,1,0:T(8,128)(2,1)S(1)} custom-call(s32[32]{0:T(128)} %prefix_ref.3, bf16[32,32,1024]{2,1,0:T(8,128)(2,1)} %bitcast.11, bf16[32,128,128]{2,1,0:T(8,128)(2,1)} %bitcast.12, bf16[32,128,128]{2,1,0:T(8,128)(2,1)} %bitcast.14, bf16[1024,2048]{1,0:T(8,128)(2,1)} %wo_hbm.1, bf16[32,32,2048]{2,1,0:T(8,128)(2,1)} %x_hbm.1, ...), custom_call_target="tpu_custom_call" | custom-call | flops 19000000512 | bytes 140000000 | tf_op jit(solution)/shard_map/pallas_call | solution.py:466
  109.6 2.0 %copy.18 = bf16[32,32,2048]{2,1,0:T(8,128)(2,1)} copy(bf16[32,32,2048]{2,1,0:T(8,128)(2,1)S(1)} %shard_map.158) | data formatting | bytes 8388608
